TPU v7x, 128 devices: a whole 4x4x4 slice. The times are simulated.
128 devices in a mesh: row: 8 (over y, z_hi), col: 16 (over z_lo, x, core).
Axes of the slice: x: 4, y: 4, z: 4 (z_hi: 2, z_lo: 2; z = z_hi * 2 + z_lo), core: 2. Of those that a mesh axis runs over, the one named last changes fastest.
Arguments:
- pair: float32 [512, 512, 128], P('row', 'col'), may hold values from -6 to 6
- valid_length: int32 [1], replicated, may hold values from 128 to 511
- tri_in: bfloat16 [128, 512], replicated, may hold values from -0.5 to 0.5
- tri_gate: bfloat16 [128, 128], replicated, may hold values from -0.5 to 0.5
- tri_out: bfloat16 [128, 128], replicated, may hold values from -0.5 to 0.5
- att_in: bfloat16 [128, 512], replicated, may hold values from -16.9705627 to 16.9705627
- att_bias: bfloat16 [128, 4], replicated, may hold values from -0.5 to 0.5
- att_out: bfloat16 [128, 128], replicated, may hold values from -0.5 to 0.5
Outputs:
- pair_out: float32 [512, 512, 128], P('row', 'col')
Inputs may be any that keep to these rules, and one draw needn't show every extreme that they name: Tokens at positions below valid_length[0] are real, the rest are padding.
All inputs are finite; a program needn't handle non-finite values.
Results may differ from a plain program's by a relative error of at most 0.025.
Values may be sent and summed in bfloat16 or wider, within the bound.
A program may use at most 128 MiB of HBM per device.

v0:
```python
import jax
import jax.numpy as jnp
from jax import lax
from jax.sharding import Mesh
from jax.sharding import PartitionSpec as P

COL = ("col_0", "col_1", "col_2")


def laid_out(tiles, dim):
    tiles = jnp.moveaxis(tiles, 0, dim)
    dims = tiles.shape
    return tiles.reshape(*dims[:dim], dims[dim] * dims[dim + 1], *dims[dim + 2 :])


def sent_to_all(value, axis):
    copies = jnp.broadcast_to(value, (lax.axis_size(axis), *value.shape))
    return lax.all_to_all(copies, axis, split_axis=0, concat_axis=0, tiled=True)


def collect(value, axis, dim):
    return laid_out(sent_to_all(value, axis), dim)


def split_up(value, dim, devices):
    before, after = (value.shape[:dim], value.shape[dim + 1 :])
    return jnp.moveaxis(value.reshape(*before, devices, -1, *after), dim, 0)


def turned_blocks(tiles, axes, turns):
    inside = tiles.shape[1:]
    filled = tiles.reshape(*(lax.axis_size(a) for a in axes), *inside)
    for k in turns:
        filled = lax.all_to_all(filled, axes[k], k, k, tiled=True)
    return filled.reshape(-1, *inside)


def exchange_by_chip(value, groups, turns, split_dim, concat_dim):
    devices = lax.axis_size(groups[0]) * lax.axis_size(groups[1])
    tiles = split_up(value, split_dim, devices)
    return laid_out(turned_blocks(tiles, groups, turns), concat_dim)


def layer_norm(values):
    center = values - jnp.mean(values, axis=-1, keepdims=True)
    return center * lax.rsqrt(jnp.mean(center * center, axis=-1, keepdims=True) + 1e-05)


def fold_keys(carry, keys_piece, values_piece, query_blocks, bias_heads, mask_bias):
    count = keys_piece.shape[1]
    nblocks, brows, cols_dev, heads, head_size = query_blocks.shape
    key_blocks = keys_piece.reshape(nblocks, brows, count, heads, head_size)
    value_blocks = values_piece.reshape(nblocks, brows, count, heads, head_size)

    def one_block(packed):
        query, keys, values, run_max, run_sum, accum = packed
        scores = jnp.einsum("ijhd,ikhd->ihjk", query, keys, preferred_element_type=jnp.float32)
        scores = scores + bias_heads[None] + mask_bias[None, None, None, :]
        new_max = jnp.maximum(run_max, jnp.max(scores, axis=-1))
        factor = jnp.exp(run_max - new_max)
        expo = jnp.exp(scores - new_max[..., None])
        new_sum = run_sum * factor + jnp.sum(expo, axis=-1)
        new_acc = accum * jnp.transpose(factor, (0, 2, 1))[..., None]
        new_acc = new_acc + jnp.einsum("ihjk,ikhd->ijhd", expo, values.astype(jnp.float32))
        return (new_max, new_sum, new_acc)

    return lax.map(one_block, (query_blocks, key_blocks, value_blocks) + tuple(carry))


def per_device(pair, valid_length, tri_in, tri_gate, tri_out, att_in, att_bias, att_out):
    rows_dev, cols_dev, width = pair.shape
    hidden = tri_out.shape[0]
    heads = att_bias.shape[1]
    head_size = width // heads
    total = cols_dev * lax.axis_size(COL)
    row_start = lax.axis_index("row") * rows_dev
    col_start = lax.axis_index(COL) * cols_dev
    tokens = jnp.arange(total)
    keep_all = (tokens < valid_length[0]).astype(jnp.float32)
    keep_rows = lax.dynamic_slice_in_dim(keep_all, row_start, rows_dev)
    keep_cols = lax.dynamic_slice_in_dim(keep_all, col_start, cols_dev)
    normed_pair = layer_norm(pair).astype(jnp.bfloat16)
    projected = jnp.dot(normed_pair, tri_in, preferred_element_type=jnp.float32)
    weight = (keep_rows[:, None] * keep_cols[None, :])[:, :, None]
    left_edges = (
        jax.nn.sigmoid(projected[..., :hidden]) * projected[..., hidden : 2 * hidden] * weight
    ).astype(jnp.bfloat16)
    right_edges = (
        jax.nn.sigmoid(projected[..., 2 * hidden : 3 * hidden])
        * projected[..., 3 * hidden :]
        * weight
    ).astype(jnp.bfloat16)
    right_rows = lax.all_gather(right_edges, "row", axis=0, tiled=True)
    swapped = lax.psum_scatter(
        jnp.einsum(
            "jkc,ikc->jic", right_rows, left_edges, preferred_element_type=jnp.float32
        ).astype(jnp.bfloat16),
        COL,
        scatter_dimension=0,
        tiled=True,
    ).astype(jnp.float32)
    normed_swapped = layer_norm(swapped).astype(jnp.bfloat16)
    tri_part = jnp.einsum(
        "jic,cd->ijd", normed_swapped, tri_out, preferred_element_type=jnp.float32
    )
    middle = (
        pair
        + jax.nn.sigmoid(jnp.dot(normed_pair, tri_gate, preferred_element_type=jnp.float32))
        * tri_part
    )
    normed_mid = layer_norm(middle).astype(jnp.bfloat16)
    bias_local = jnp.dot(normed_mid, att_bias, preferred_element_type=jnp.float32).astype(
        jnp.bfloat16
    )
    bias_rows = collect(bias_local, "row", 0)
    bias_cols = exchange_by_chip(bias_rows, (("col_0", "col_1"), "col_2"), (1, 0), 0, 1)
    bias_heads = jnp.transpose(bias_cols.astype(jnp.float32), (2, 0, 1))
    mask_bias = jnp.where(tokens < valid_length[0], 0.0, -1000000000.0).astype(jnp.float32)
    nblocks = rows_dev // 8
    query = (
        jnp.dot(normed_mid, att_in[:, :width], preferred_element_type=jnp.float32)
        * head_size ** (-0.5)
    ).astype(jnp.bfloat16)
    query_blocks = query.reshape(nblocks, 8, cols_dev, heads, head_size)
    gate = jax.nn.sigmoid(
        jnp.dot(normed_mid, att_in[:, 3 * width :], preferred_element_type=jnp.float32)
    )
    start_state = (
        jnp.full((nblocks, 8, heads, cols_dev), -1e30, jnp.float32),
        jnp.zeros((nblocks, 8, heads, cols_dev), jnp.float32),
        jnp.zeros((nblocks, 8, cols_dev, heads, head_size), jnp.float32),
    )
    made = jnp.dot(
        lax.all_gather(normed_mid, COL, axis=1, tiled=True),
        att_in[:, width : 3 * width],
        preferred_element_type=jnp.float32,
    )
    keys_piece = made[..., :width].astype(jnp.bfloat16)
    values_piece = made[..., width:].astype(jnp.bfloat16)
    state = fold_keys(start_state, keys_piece, values_piece, query_blocks, bias_heads, mask_bias)
    run_sum = state[1]
    accum = state[2]
    attended = accum / jnp.transpose(run_sum, (0, 1, 3, 2))[..., None]
    attended = attended.reshape(rows_dev, cols_dev, width)
    gated = (gate * attended).astype(jnp.bfloat16)
    return middle + jnp.dot(gated, att_out, preferred_element_type=jnp.float32)


def solution(mesh):
    torus = Mesh(
        mesh.devices.reshape(mesh.shape["row"], 2, 4, 2), ("row", "col_0", "col_1", "col_2")
    )
    placed = (P("row", COL, None), P(), P(), P(), P(), P(), P(), P())
    return jax.shard_map(
        per_device, mesh=torus, in_specs=placed, out_specs=P("row", COL, None), check_vma=False
    )
```

profile of v0, /device:TPU:33, one launch (start us, length us, event | category | flops | bytes accessed | tf_op | source)
XLA Modules:
  0.0 339.2 jit_solution(4258924247449309692)
XLA Ops:
  9.0 1.9 multiply_reduce_fusion.1
  10.9 2.1 fusion.46
  16.2 70.5 %all-gather.3.cloned.1.call-done = bf16[512,32,128]{2,1,0:T(8,128)(2,1)} async-done(((bf16[64,32,128]{2,1,0:T(8,128)(2,1)}), bf16[512,32,128]{2,1,0:T(8,128)(2,1)}) %all-gather.3.cloned.1.call-update) | async-done | bytes 4194320 | tf_op jit(solution)/shard_map/all_gather | solution.py:93
  86.6 8.5 %copy.43 = bf16[512,32,128]{0,1,2:T(8,128)(2,1)} copy(bf16[512,32,128]{2,1,0:T(8,128)(2,1)} %all-gather.3.cloned.1.call-done) | data formatting | bytes 8388608 | tf_op jit(solution)/shard_map/all_gather | solution.py:93
  95.2 7.8 %convert_bitcast_fusion = bf16[512,64,128]{0,1,2:T(8,128)(2,1)} fusion(bf16[64,32,128]{0,1,2:T(8,128)(2,1)S(1)} %copy.42, bf16[512,32,128]{0,1,2:T(8,128)(2,1)} %copy.43), kind=kOutput, calls=%fused_computation.29 | convolution fusion | flops 272629760 | bytes 13107200 | tf_op jit(solution)/shard_map/jkc,ikc->jic/dot_general | solution.py:95
  103.0 13.7 %copy.44 = bf16[512,64,128]{2,1,0:T(8,128)(2,1)} copy(bf16[512,64,128]{0,1,2:T(8,128)(2,1)} %convert_bitcast_fusion) | data formatting | bytes 16777216 | tf_op jit(solution)/shard_map/convert_element_type | solution.py:97
  116.7 70.3 %reduce-scatter.2.cloned.1.call-done = bf16[32,64,128]{2,1,0:T(8,128)(2,1)} async-done(((bf16[512,64,128]{2,1,0:T(8,128)(2,1)}), bf16[32,64,128]{2,1,0:T(8,128)(2,1)}) %reduce-scatter.2.cloned.1.call-update) | async-done | bytes 524304 | tf_op jit(solution)/shard_map/reduce_scatter | solution.py:94
  196.4 1.9 convolution_convert_fusion.1
  199.3 5.5 %all-to-all-start = ((bf16[8,2,4096]{2,1,0:T(2,128)(2,1)}), bf16[8,2,4096]{2,1,0:T(2,128)(2,1)S(1)}, u32[]{:S(2)}, u32[]{:S(2)}) async-start(bf16[8,2,4096]{2,1,0:T(2,128)(2,1)} %reshape.134), calls=%async_computation.1 | async-start | bytes 262144 | tf_op jit(solution)/shard_map/all_to_all | solution.py:18
  204.9 6.9 %all-to-all-done = bf16[8,2,4096]{2,1,0:T(2,128)(2,1)S(1)} async-done(((bf16[8,2,4096]{2,1,0:T(2,128)(2,1)}), bf16[8,2,4096]{2,1,0:T(2,128)(2,1)S(1)}, u32[]{:S(2)}, u32[]{:S(2)}) %all-to-all-start) | async-done | bytes 131104 | tf_op jit(solution)/shard_map/all_to_all | solution.py:18
  212.8 8.8 %all_to_all.15 = bf16[2,2,16384]{2,1,0:T(2,128)(2,1)S(1)} all-to-all(bf16[2,2,16384]{2,1,0:T(2,128)(2,1)S(1)} %reshape.136), channel_id=1, replica_groups=mesh['row'=8,'col_0'=2,'col_1'=4,'col_2'=2] {'col_2'}, dimensions={0} | all-to-all | bytes 262144 | tf_op jit(solution)/shard_map/all_to_all | solution.py:34
  223.3 5.1 %all-to-all-start.2 = ((bf16[8,2,4096]{2,1,0:T(2,128)(2,1)}), bf16[8,2,4096]{2,1,0:T(2,128)(2,1)S(1)}, u32[]{:S(2)}, u32[]{:S(2)}) async-start(bf16[8,2,4096]{2,1,0:T(2,128)(2,1)} %reshape.138), calls=%async_computation.3 | async-start | bytes 262144 | tf_op jit(solution)/shard_map/all_to_all | solution.py:34
  230.3 3.2 all-to-all-done.2
  237.3 15.6 %all-gather.5.cloned.1.call-done = bf16[64,512,128]{2,1,0:T(8,128)(2,1)} async-done(((bf16[64,32,128]{2,1,0:T(8,128)(2,1)}), bf16[64,512,128]{2,1,0:T(8,128)(2,1)}) %all-gather.5.cloned.1.call-update) | async-done | bytes 8388624 | tf_op jit(solution)/shard_map/all_gather | solution.py:134
  252.9 10.5 %convolution_convert_fusion = bf16[64,512,256]{1,2,0:T(8,128)(2,1)} fusion(bf16[64,512,128]{2,1,0:T(8,128)(2,1)} %all-gather.5.cloned.1.call-done, bf16[128,512]{1,0:T(8,128)(2,1)} %param.15), kind=kOutput, calls=%fused_computation.28 | convolution fusion | flops 2155872256 | bytes 25231360 | tf_op jit(solution)/shard_map/dot_general | solution.py:133
  263.4 11.6 %fusion.68 = (bf16[64,512,128]{1,2,0:T(8,128)(2,1)}, bf16[64,512,128]{1,2,0:T(8,128)(2,1)}) fusion(bf16[64,512,256]{1,2,0:T(8,128)(2,1)} %convolution_convert_fusion), kind=kLoop, calls=%fused_computation.101 | loop fusion | bytes 33554432 | tf_op jit(solution)/shard_map/slice | solution.py:139
  275.0 47.4 %while.13 = (s32[]{:T(128)}, f32[8,8,4,32]{3,2,1,0:T(4,128)S(1)}, f32[8,8,32,4,32]{2,4,3,1,0:T(8,128)}, bf16[8,8,32,4,32]{4,3,2,1,0:T(4,128)(2,1)S(1)}, bf16[8,8...) while((s32[]{:T(128)}, f32[8,8,4,32]{3,2,1,0:T(4,128)S(1)}, ...), condition=%wide.region_10.11_spmd.clone, body=%wide.region_7.10_spmd.clone.sunk | while | flops 72390656 | bytes 9987689 | solution.py:67
  275.8 1.7 fusion.84
  277.6 2.7 fusion.87
  283.5 2.7 fusion.87
  289.4 2.7 fusion.87
  295.3 2.7 fusion.87
  299.5 1.8 fusion.84
  301.3 2.7 fusion.87
  305.4 1.7 fusion.84
  307.2 2.7 fusion.87
  311.4 1.7 fusion.84
  313.2 2.7 fusion.87
  319.1 2.7 fusion.87
  322.5 5.0 %broadcast_divide_fusion = f32[8,8,32,4,32]{2,4,3,1,0:T(8,128)} fusion(f32[8,8,32,4,32]{2,4,3,1,0:T(8,128)} %get-tuple-element.48, f32[8,8,32,4]{2,3,1,0:T(4,128)S(1)} %bitcast.119), kind=kLoop, calls=%fused_computation.30 | loop fusion | flops 262144 | bytes 2129920 | tf_op jit(solution)/shard_map/div | solution.py:143
  327.5 2.9 copy.53
  330.4 2.3 convolution_add_fusion
  (110 shorter events, 42.3 us)
Async XLA Ops:
  6.5 4.4 %copy-start = (bf16[128,512]{1,0:T(8,128)(2,1)S(1)}, bf16[128,512]{1,0:T(8,128)(2,1)}, u32[]{:S(2)}) copy-start(bf16[128,512]{1,0:T(8,128)(2,1)} %param.12) | copy-start | bytes 393220
  6.5 80.1 %all-gather.3.cloned.1.call-start = ((), (), s32[]{:S(2)}) async-start(), calls=%async_computation.4 | async-start | bytes 4718592 | tf_op jit(solution)/shard_map/all_gather | solution.py:93
  14.4 172.7 %reduce-scatter.2.cloned.1.call-start = ((), (), s32[]{:S(2)}) async-start(), calls=%async_computation.5 | async-start | bytes 8912896 | tf_op jit(solution)/shard_map/reduce_scatter | solution.py:94
  116.6 75.2 %copy-start.7 = (bf16[128,128]{1,0:T(8,128)(2,1)S(1)}, bf16[128,128]{1,0:T(8,128)(2,1)}, u32[]{:S(2)}) copy-start(bf16[128,128]{1,0:T(8,128)(2,1)} %param.14) | copy-start | bytes 98308
  116.6 75.6 %copy-start.2 = (f32[64,32,128]{2,1,0:T(8,128)S(1)}, f32[64,32,128]{2,1,0:T(8,128)}, u32[]{:S(2)}) copy-start(f32[64,32,128]{2,1,0:T(8,128)} %param.10) | copy-start | bytes 3145732
  116.6 75.6 %copy-start.9 = (bf16[128,128]{1,0:T(8,128)(2,1)S(1)}, bf16[128,128]{1,0:T(8,128)(2,1)}, u32[]{:S(2)}) copy-start(bf16[128,128]{1,0:T(8,128)(2,1)} %param.13) | copy-start | bytes 98308
  116.7 136.3 %all-gather.5.cloned.1.call-start = ((), (), s32[]{:S(2)}) async-start(), calls=%async_computation.6 | async-start | bytes 8912896 | tf_op jit(solution)/shard_map/all_gather | solution.py:134
  192.2 4.2 %copy-start.8 = (bf16[128,4]{0,1:T(4,128)(2,1)S(1)}, bf16[128,4]{0,1:T(4,128)(2,1)}, u32[]{:S(2)}) copy-start(bf16[128,4]{0,1:T(4,128)(2,1)} %param.16) | copy-start | bytes 3076
  194.0 1.0 copy-start.4
  196.4 32.0 %copy-start.3 = (bf16[64,32,128]{2,1,0:T(8,128)(2,1)S(1)}, bf16[64,32,128]{2,1,0:T(8,128)(2,1)}, u32[]{:S(2)}) copy-start(bf16[64,32,128]{2,1,0:T(8,128)(2,1)} %multiply_convert_fusion) | copy-start | bytes 1572868
  199.3 12.4 %all-to-all-start = ((bf16[8,2,4096]{2,1,0:T(2,128)(2,1)}), bf16[8,2,4096]{2,1,0:T(2,128)(2,1)S(1)}, u32[]{:S(2)}, u32[]{:S(2)}) async-start(bf16[8,2,4096]{2,1,0:T(2,128)(2,1)} %reshape.134), calls=%async_computation.1 | async-start | bytes 262144 | tf_op jit(solution)/shard_map/all_to_all | solution.py:18
  223.3 10.2 %all-to-all-start.2 = ((bf16[8,2,4096]{2,1,0:T(2,128)(2,1)}), bf16[8,2,4096]{2,1,0:T(2,128)(2,1)S(1)}, u32[]{:S(2)}, u32[]{:S(2)}) async-start(bf16[8,2,4096]{2,1,0:T(2,128)(2,1)} %reshape.138), calls=%async_computation.3 | async-start | bytes 262144 | tf_op jit(solution)/shard_map/all_to_all | solution.py:34
  263.4 11.6 %copy-start.6 = (f32[8,8,4,32]{3,2,1,0:T(4,128)S(1)}, f32[8,8,4,32]{3,2,1,0:T(4,128)}, u32[]{:S(2)}) copy-start(f32[8,8,4,32]{3,2,1,0:T(4,128)} %custom-call) | copy-start | bytes 98308
  327.5 2.9 copy-start.5
  327.5 2.9 copy-start.10
  327.5 5.2 %copy-start.1 = (bf16[128,512]{1,0:T(8,128)(2,1)S(1)}, bf16[128,512]{1,0:T(8,128)(2,1)}, u32[]{:S(2)}) copy-start(bf16[128,512]{1,0:T(8,128)(2,1)} %param.12) | copy-start | bytes 393220
Sparse Core Ops, SparseCore 0:
  14.5 72.0 all-gather.2
  116.8 70.2 reduce-scatter.1
  196.5 56.3 all-gather.4
where the time goes:
time: 343 us; the launch traced here: 339 us
  waiting for transfers between devices  167 us (49%)
  matrix products  63.1 us (18%)
  local copies, waits for them, and re-layouts  48 us (14%)
  other arithmetic  27.7 us (8%)
  between operations  14.1 us (4%)
  starting transfers between devices  10.7 us (3%)
  blocking collectives  8.77 us (3%)
    all_gather x1, waiting for transfers between devices, per_device(): right_rows = lax.all_gather(right_edges, 'row', axis=0, tiled=True)  70.5 us
    reduce_scatter x1, waiting for transfers between devices, per_device(): lax.psum_scatter(jnp.einsum('jkc,ikc->jic', right_rows, left_edges, prefe...  70.3 us
    dot_general x8, matrix products, one_block(): jnp.einsum('ihjk,ikhd->ijhd', expo, values.astype(jnp.float32))  21.6 us
    all_gather x1, waiting for transfers between devices, per_device(): lax.all_gather(normed_mid, COL, axis=1, tiled=True)  15.6 us
    dot_general x8, matrix products, one_block(): jnp.einsum('ijhd,ikhd->ihjk', query, keys, preferred_element_type=jnp.flo...  13.9 us
    convert_element_type x1, local copies, waits for them, and re-layouts, per_device(): swapped = lax.psum_scatter(jnp.einsum('jkc,ikc->jic', right_rows, left_ed...  13.7 us
    slice x1, local copies, waits for them, and re-layouts, per_device(): values_piece = made[..., width:].astype(jnp.bfloat16)  11.6 us
    dot_general x1, matrix products, per_device(): jnp.dot(lax.all_gather(normed_mid, COL, axis=1, tiled=True), att_in[:, wi...  10.5 us
  transfers between devices with their start and end apart: 5, of which 5 were waited for; matrix products, arithmetic and copies ran while one was open for 4% of the time, Pallas kernels for 0%

commit v1 on v0

v1 whole, which is shorter than its diff:
```python
import functools

import jax
import jax.numpy as jnp
from jax import lax
from jax.experimental import pallas as pl
from jax.experimental.pallas import tpu as pltpu
from jax.sharding import PartitionSpec as P

MESH = pl.DeviceIdType.MESH
F32 = jnp.float32
BF16 = jnp.bfloat16
NT = (((1,), (1,)), ((), ()))
TN = (((0,), (0,)), ((), ()))
NN = (((1,), (0,)), ((), ()))


def dot(a, b, dims=NN):
    return lax.dot_general(a, b, dims, preferred_element_type=F32)


def norm_last(x):
    c = x - jnp.mean(x, axis=-1, keepdims=True)
    return c * lax.rsqrt(jnp.mean(c * c, axis=-1, keepdims=True) + 1e-5)


def turned(w):
    return w.astype(F32).T.astype(BF16)


def swap16():
    p = lax.broadcasted_iota(jnp.int32, (256, 256), 0)
    q = lax.broadcasted_iota(jnp.int32, (256, 256), 1)
    return (q == (p % 16) * 16 + p // 16).astype(F32).astype(BF16)


def block_turn(tiles):
    return [
        jnp.concatenate([t[:, 32 * b : 32 * b + 32] for t in tiles], axis=1) for b in range(4)
    ]


def tile_of(x_ref, s):
    return jnp.concatenate([x_ref[16 * b + s] for b in range(4)], axis=0)


def edges_body(x_ref, len_ref, tri_in_ref, e_ref, n_ref, wt, y):
    wt[...] = turned(tri_in_ref[...])
    row = lax.axis_index("row") * 64
    col = lax.axis_index("col") * 32
    lane = lax.broadcasted_iota(jnp.int32, (1, 128), 1)
    length = len_ref[0]
    keep_k = (col + lane % 32) < length

    def one(s, _):
        nb = norm_last(tile_of(x_ref, s)).astype(BF16)
        n_ref[s] = nb
        pt = dot(wt[...], nb, NT)
        w = jnp.where(keep_k & ((row + (lane // 32) * 16 + s) < length), 1.0, 0.0)
        for side in range(2):
            g = pt[256 * side : 256 * side + 128]
            v = pt[256 * side + 128 : 256 * side + 256]
            edge = (jax.nn.sigmoid(g) * v * w).astype(BF16)
            y[:, pl.ds(pl.multiple_of(16 * s, 16), 16), 128 * side : 128 * side + 128] = (
                edge.reshape(8, 16, 128)
            )
        return 0

    lax.fori_loop(0, 16, one, 0)
    perm = swap16()

    def group(g, _):
        z = dot(perm, y[g]).astype(BF16)
        at = pl.ds(pl.multiple_of(16 * g, 16), 16)
        e_ref[at, 0] = z[:, :128].reshape(16, 16, 128)
        e_ref[at, 1] = z[:, 128:].reshape(16, 16, 128)
        return 0

    lax.fori_loop(0, 8, group, 0)


def triangle_body(rx_ref, o_ref, lm, rm):
    def gather(r, _):
        for side, m in ((0, lm), (1, rm)):
            for cg in range(4):
                tiles = [rx_ref[16 * r + 4 * cg + c, side] for c in range(4)]
                for b, t in enumerate(block_turn(tiles)):
                    at = pl.ds(pl.multiple_of(64 * r + 16 * b, 16), 16)
                    m[at, 128 * cg : 128 * cg + 128] = t
        return 0

    lax.fori_loop(0, 8, gather, 0)

    def rows(r, _):
        p = dot(lm[pl.ds(pl.multiple_of(64 * r, 64), 64), :], rm[...], NT).astype(BF16)
        for cg in range(4):
            tiles = [p[16 * b : 16 * b + 16, 128 * cg : 128 * cg + 128] for b in range(4)]
            for c, t in enumerate(block_turn(tiles)):
                o_ref[16 * r + 4 * cg + c] = t
        return 0

    lax.fori_loop(0, 8, rows, 0)


def middle_body(x_ref, n_ref, px_ref, gate_ref, out_ref, bias_ref, mid_ref, nm_ref, bm_ref, np_, yb):
    total = lax.fori_loop(
        0, 128, lambda c, a: a + px_ref[c].astype(F32), jnp.zeros((16, 128), F32), unroll=8
    )
    mean = total * (1.0 / 128)

    def square(c, a):
        d = px_ref[c].astype(F32) - mean
        return a + d * d

    var = lax.fori_loop(0, 128, square, jnp.zeros((16, 128), F32), unroll=8) * (1.0 / 128)
    scale = lax.rsqrt(var + 1e-5)
    perm = swap16()

    def group(g, _):
        at = pl.ds(pl.multiple_of(16 * g, 16), 16)
        z = ((px_ref[at].astype(F32) - mean[None]) * scale[None]).astype(BF16)
        z = dot(perm, z.reshape(256, 128)).astype(BF16)
        np_[:, at, :] = z.reshape(16, 16, 128)
        return 0

    lax.fori_loop(0, 8, group, 0)
    wb = bias_ref[...]

    def one(s, _):
        tri = dot(np_[s], out_ref[...], TN)
        gate = jax.nn.sigmoid(dot(n_ref[s], gate_ref[...]))
        mid = tile_of(x_ref, s) + gate * tri
        mid_ref[s] = mid
        nm = norm_last(mid).astype(BF16)
        nm_ref[s] = nm
        yb[pl.ds(s, 8, stride=16), :] = dot(wb, nm, NT)
        return 0

    lax.fori_loop(0, 16, one, 0)
    yt = yb[...].T
    bm_ref[...] = jnp.concatenate([yt[32 * b : 32 * b + 32, :64] for b in range(4)], axis=1).astype(
        BF16
    )


def attend_body(nx_ref, bx_ref, len_ref, att_in_ref, go_ref, qs, ks, vt, gt, bias, tile):
    wvt = turned(att_in_ref[:, 256:384])
    wgt = turned(att_in_ref[:, 384:512])
    lane128 = lax.broadcasted_iota(jnp.int32, (1, 128), 1)
    kk = lax.broadcasted_iota(jnp.int32, (512, 256), 0)
    mask = jnp.where(kk < len_ref[0], 0.0, -1e9).astype(F32).reshape(8, 2, 32, 256)

    def project(c, _):
        nx = nx_ref[c]
        qk = dot(nx, att_in_ref[:, :256])
        qs[c] = (qk[:, :128] * 32 ** (-0.5)).astype(BF16)
        ks[c] = qk[:, 128:].astype(BF16)
        gt[c] = jax.nn.sigmoid(dot(wgt, nx, NT))
        return 0

    lax.fori_loop(0, 16, project, 0)
    for b in range(4):
        rows = nx_ref[:, 32 * b : 32 * b + 32, :].reshape(512, 128)
        vt[b, :128] = dot(wvt, rows, NT).astype(BF16)
        vt[b, 128:] = jnp.ones((16, 512), BF16)

    def block(r, _):
        for core in range(2):
            got = bx_ref[core, pl.ds(pl.multiple_of(8 * r, 8), 8)].astype(F32)
            bias[:, core] = got + mask[:, core]
        for b in range(4):
            q = qs[pl.ds(2 * r, 2), 32 * b : 32 * b + 32, :].reshape(4, 1, 16, 128)
            hd = lax.broadcasted_iota(jnp.int32, (4, 4, 16, 128), 1)
            ln = lax.broadcasted_iota(jnp.int32, (4, 4, 16, 128), 3)
            qm = jnp.where(
                hd == ln // 32, jnp.broadcast_to(q, (4, 4, 16, 128)).astype(F32), 0.0
            ).astype(BF16)
            keys = ks[:, 32 * b : 32 * b + 32, :].reshape(512, 128)
            st = dot(keys, qm.reshape(256, 128), NT) + bias[...].reshape(512, 256)
            p = jnp.exp(st - jnp.max(st, axis=0, keepdims=True)).astype(BF16)
            ot = dot(vt[b], p)
            ot = ot[:128] / ot[128:129]
            for h in range(4):
                part = ot[32 * h : 32 * h + 32]
                for j in range(4):
                    at = 64 * (j % 2) + 16 * h
                    to = 32 * b + 16 * (j % 2)
                    moved = part[:, 128 * (j // 2) : 128 * (j // 2) + 128]
                    if (to - at) % 128:
                        moved = pltpu.roll(moved, (to - at) % 128, 1)
                    here = (lane128 >= to) & (lane128 < to + 16)
                    rows = slice(32 * h, 32 * h + 32)
                    tile[j // 2, rows] = jnp.where(here, moved, tile[j // 2, rows])
        for c in range(2):
            go_ref[2 * r + c] = (tile[c] * gt[2 * r + c]).astype(BF16)
        return 0

    tile[...] = jnp.zeros((2, 128, 128), F32)
    lax.fori_loop(0, 8, block, 0)


def final_body(gx_ref, mid_ref, att_out_ref, y_ref):
    def one(s, _):
        y = mid_ref[s] + dot(gx_ref[s], att_out_ref[...], TN)
        for b in range(4):
            y_ref[16 * b + s] = y[32 * b : 32 * b + 32]
        return 0

    lax.fori_loop(0, 16, one, 0)


VMEM = pl.BlockSpec(memory_space=pltpu.VMEM)
SMEM = pl.BlockSpec(memory_space=pltpu.SMEM)
LIMIT = 60 * 1024 * 1024


def call(body, outs, ins, scratch=(), smem=(), **params):
    many = isinstance(outs, list)
    return pl.pallas_call(
        body,
        out_shape=[jax.ShapeDtypeStruct(*o) for o in outs] if many else jax.ShapeDtypeStruct(*outs),
        in_specs=[SMEM if n in smem else VMEM for n in range(len(ins))],
        out_specs=[VMEM] * len(outs) if many else VMEM,
        scratch_shapes=list(scratch),
        compiler_params=pltpu.CompilerParams(vmem_limit_bytes=LIMIT, **params),
    )(*ins)


def spread_body(x_ref, o_ref, send_sem, near_sem, far_sem):
    r, c = lax.axis_index("row"), lax.axis_index("col")
    core = c % 2
    mate = c + 1 - 2 * core
    bar = pltpu.get_barrier_semaphore()

    def peer(k):
        return (lax.rem(r + k // 8, 8), 2 * lax.rem(c // 2 + k % 8, 8) + core)

    def greet(k, _):
        pl.semaphore_signal(bar, inc=1, device_id=peer(k), device_id_type=MESH)
        return 0

    lax.fori_loop(1, 64, greet, 0)
    pl.semaphore_signal(bar, inc=1, device_id=(r, mate), device_id_type=MESH)
    pl.semaphore_wait(bar, 64)

    def send(k, _):
        pltpu.make_async_remote_copy(
            x_ref, o_ref.at[core, 8 * r + c // 2], send_sem, near_sem, peer(k), MESH
        ).start()
        return 0

    lax.fori_loop(1, 64, send, 0)
    o_ref[core, 8 * r + c // 2] = x_ref[...]
    most = o_ref.at[0, pl.ds(0, 63)]
    pltpu.make_async_copy(most, most, near_sem).wait()
    pltpu.make_async_copy(most, most, send_sem).wait()
    mine = o_ref.at[core]
    copy = pltpu.make_async_remote_copy(mine, mine, send_sem, far_sem, (r, mate), MESH)
    copy.start()
    copy.wait()


def per_device(pair, valid_length, tri_in, tri_gate, tri_out, att_in, att_bias, att_out):
    both = ("row", "col")
    bias8 = jnp.pad(att_bias.T, ((0, 4), (0, 0)))
    edges, normed = call(
        edges_body,
        [((128, 2, 16, 128), BF16), ((16, 128, 128), BF16)],
        (pair, valid_length, tri_in),
        [pltpu.VMEM((512, 128), BF16), pltpu.VMEM((8, 256, 256), BF16)],
        smem=(1,),
    )
    got = lax.all_to_all(edges, both, 0, 0, tiled=True)
    products = call(
        triangle_body,
        ((128, 16, 128), BF16),
        (got,),
        [pltpu.VMEM((512, 512), BF16), pltpu.VMEM((512, 512), BF16)],
    )
    home = lax.all_to_all(products, both, 0, 0, tiled=True)
    middle, mid_norm, bias = call(
        middle_body,
        [((16, 128, 128), F32), ((16, 128, 128), BF16), ((32, 256), BF16)],
        (pair, normed, home, tri_gate, tri_out, bias8),
        [pltpu.VMEM((16, 128, 128), BF16), pltpu.VMEM((128, 128), F32)],
    )
    rows = lax.all_to_all(mid_norm, "col", 0, 0, tiled=True)
    bias_all = call(
        spread_body,
        ((2, 64, 32, 256), BF16),
        (bias,),
        [pltpu.SemaphoreType.DMA] * 3,
        collective_id=1,
        has_side_effects=True,
    )
    gated = call(
        attend_body,
        ((16, 128, 128), BF16),
        (rows, bias_all, valid_length, att_in),
        [
            pltpu.VMEM((16, 128, 128), BF16),
            pltpu.VMEM((16, 128, 128), BF16),
            pltpu.VMEM((4, 144, 512), BF16),
            pltpu.VMEM((16, 128, 128), F32),
            pltpu.VMEM((8, 2, 32, 256), F32),
            pltpu.VMEM((2, 128, 128), F32),
        ],
        smem=(2,),
    )
    back = lax.all_to_all(gated, "col", 0, 0, tiled=True)
    return call(final_body, ((64, 32, 128), F32), (back, middle, att_out))


def solution(mesh):
    placed = (P("row", "col", None), P(), P(), P(), P(), P(), P(), P())
    return jax.shard_map(
        per_device, mesh=mesh, in_specs=placed, out_specs=P("row", "col", None), check_vma=False
    )
```

time: 343 us -> 152 us (0.44)
  waiting for transfers between devices: 167 us -> 11.4 us
  Pallas kernels: 0 us -> 81.1 us
  matrix products: 63.1 us -> 0 us
  local copies, waits for them, and re-layouts: 48 us -> 2.17 us
  blocking collectives: 8.77 us -> 42.1 us
  other arithmetic: 27.7 us -> 0 us
  between operations: 14.1 us -> 0.7 us
    all_gather x2 -> x0, waiting for transfers between devices: 86.1 us -> none  [the longest x1 70.5 us: per_device(): right_rows = lax.all_gather(right_edges, 'row', axis=0, tiled=True)]
    pallas_call x0 -> x6, Pallas kernels: none -> 81.1 us  [call(): pl.pallas_call(body, out_shape=[jax.ShapeDtypeStruct(*o) for o in outs] i...]
    reduce_scatter x1 -> x0, waiting for transfers between devices: 70.3 us -> none  [per_device(): lax.psum_scatter(jnp.einsum('jkc,ikc->jic', right_rows, left_edges, prefe...]
    dot_general x24 -> x0, matrix products: 63.1 us -> none  [the longest x8 21.6 us: one_block(): jnp.einsum('ihjk,ikhd->ijhd', expo, values.astype(jnp.float32))]
    all_to_all x1 -> x2, blocking collectives: 8.77 us -> 42.1 us  [the longest x1 27.8 us: per_device(): got = lax.all_to_all(edges, both, 0, 0, tiled=True)]
    convert_element_type x3 -> x0, local copies, waits for them, and re-layouts: 15.5 us -> none  [the longest x1 13.7 us: per_device(): swapped = lax.psum_scatter(jnp.einsum('jkc,ikc->jic', right_rows, left_ed...]
    reduce_sum x13 -> x0, other arithmetic: 12.4 us -> none  [the longest x8 5.24 us: one_block(): new_sum = run_sum * factor + jnp.sum(expo, axis=-1)]
    slice x1 -> x0, local copies, waits for them, and re-layouts: 11.6 us -> none  [per_device(): values_piece = made[..., width:].astype(jnp.bfloat16)]
  transfers between devices with their start and end apart: 5 -> 2, of which waited for: 5 -> 1; matrix products, arithmetic and copies ran while one was open for 4% -> 0% of each run, Pallas kernels for 0% -> 18%
where the time goes in v1:
time: 152 us; the launch traced here: 150 us
  Pallas kernels  81.1 us (53%)
  blocking collectives  42.1 us (28%)
  starting transfers between devices  12.5 us (8%)
  waiting for transfers between devices  11.4 us (8%)
  local copies, waits for them, and re-layouts  2.17 us (1%)
    pallas_call x6, Pallas kernels, call(): pl.pallas_call(body, out_shape=[jax.ShapeDtypeStruct(*o) for o in outs] i...  81.1 us
    all_to_all x1, blocking collectives, per_device(): got = lax.all_to_all(edges, both, 0, 0, tiled=True)  27.8 us
    all_to_all x1, blocking collectives, per_device(): back = lax.all_to_all(gated, 'col', 0, 0, tiled=True)  14.3 us
    all_to_all x1, waiting for transfers between devices, per_device(): home = lax.all_to_all(products, both, 0, 0, tiled=True)  11.4 us
    all_to_all x1, starting transfers between devices, per_device(): home = lax.all_to_all(products, both, 0, 0, tiled=True)  6.58 us
    all_to_all x1, starting transfers between devices, per_device(): rows = lax.all_to_all(mid_norm, 'col', 0, 0, tiled=True)  5.89 us
  transfers between devices with their start and end apart: 2, of which 1 were waited for; matrix products, arithmetic and copies ran while one was open for 0% of the time, Pallas kernels for 18%

profile of v1, /device:TPU:33, one launch (start us, length us, event | category | flops | bytes accessed | tf_op | source)
XLA Modules:
  0.0 149.9 jit_solution(17204530732279763090)
XLA Ops:
  0.7 9.6 %shard_map.82 = (bf16[128,2,16,128]{3,2,1,0:T(8,128)(2,1)}, bf16[16,128,128]{2,1,0:T(8,128)(2,1)}) custom-call(f32[64,32,128]{2,1,0:T(8,128)} %x_ref.3, s32[1]{0:T(128)S(6)} %copy.9.len_ref, bf16[128,512]{1,0:T(8,128)(2,1)} %tri_in_ref.1), custom_call_target="tpu_custom_call" | custom-call | tf_op jit(solution)/shard_map/pallas_call | solution.py:219
  10.2 0.0 copy-start.2
  10.2 27.8 %all_to_all.20.rx_ref = bf16[128,2,16,128]{3,2,1,0:T(8,128)(2,1)} all-to-all(bf16[128,2,16,128]{3,2,1,0:T(8,128)(2,1)} %get-tuple-element.11), channel_id=1, replica_groups=mesh['row'=8,'col'=16] {'row','col'}, dimensions={0} | all-to-all | bytes 2097152 | tf_op jit(solution)/shard_map/all_to_all | solution.py:273
  38.0 6.5 %shard_map.83 = bf16[128,16,128]{2,1,0:T(8,128)(2,1)} custom-call(bf16[128,2,16,128]{3,2,1,0:T(8,128)(2,1)} %all_to_all.20.rx_ref), custom_call_target="tpu_custom_call" | custom-call | tf_op jit(solution)/shard_map/pallas_call | solution.py:219
  44.5 6.6 %all-to-all-start.1 = ((bf16[128,16,128]{2,1,0:T(8,128)(2,1)}), bf16[128,16,128]{2,1,0:T(8,128)(2,1)S(1)}, u32[]{:S(2)}, u32[]{:S(2)}) async-start(bf16[128,16,128]{2,1,0:T(8,128)(2,1)} %shard_map.83), calls=%async_computation.1 | async-start | bytes 1048576 | tf_op jit(solution)/shard_map/all_to_all | solution.py:280
  51.1 0.0 copy-done.2
  51.1 0.6 pad.4.bias_ref
  51.7 11.4 %all-to-all-done.1.px_ref = bf16[128,16,128]{2,1,0:T(8,128)(2,1)S(1)} async-done(((bf16[128,16,128]{2,1,0:T(8,128)(2,1)}), bf16[128,16,128]{2,1,0:T(8,128)(2,1)S(1)}, u32[]{:S(2)}, u32[]{:S(2)}) %all-to-all-start.1) | async-done | bytes 524320 | tf_op jit(solution)/shard_map/all_to_all | solution.py:280
  63.1 0.0 copy-start
  63.1 0.8 copy-done
  63.8 12.5 %shard_map.84 = (f32[16,128,128]{2,1,0:T(8,128)}, bf16[16,128,128]{2,1,0:T(8,128)(2,1)}, bf16[32,256]{1,0:T(8,128)(2,1)}) custom-call(f32[64,32,128]{2,1,0:T(8,128)} %x_ref.3, bf16[16,128,128]{2,1,0:T(8,128)(2,1)} %get-tuple-element.10.n_ref, bf16[128,16,128]{2,1,0:T(8,128)(2,1)} %copy-done, bf16[128,128]{1,0:T(8,128)(2,1)} %gate_ref.1, ...), custom_call_target="tpu_custom_call" | custom-call | tf_op jit(solution)/shard_map/pallas_call | solution.py:219
  76.4 5.9 %all-to-all-start.2 = ((bf16[16,128,128]{2,1,0:T(8,128)(2,1)}), bf16[16,128,128]{2,1,0:T(8,128)(2,1)S(1)}, u32[]{:S(2)}, u32[]{:S(2)}) async-start(bf16[16,128,128]{2,1,0:T(8,128)(2,1)} %get-tuple-element.12), calls=%async_computation.2 | async-start | bytes 1048576 | tf_op jit(solution)/shard_map/all_to_all | solution.py:287
  82.3 26.6 %shard_map.85.bx_ref = bf16[2,64,32,256]{3,2,1,0:T(8,128)(2,1)} custom-call(bf16[32,256]{1,0:T(8,128)(2,1)} %get-tuple-element.13.x_ref), custom_call_target="tpu_custom_call" | custom-call | tf_op jit(solution)/shard_map/pallas_call | solution.py:219
  108.9 0.0 all-to-all-done.2.nx_ref
  108.9 0.0 copy-start.1
  108.9 0.8 copy-done.1
  109.7 20.6 %shard_map.86 = bf16[16,128,128]{2,1,0:T(8,128)(2,1)} custom-call(bf16[16,128,128]{2,1,0:T(8,128)(2,1)} %copy-done.1, bf16[2,64,32,256]{3,2,1,0:T(8,128)(2,1)} %shard_map.85.bx_ref, s32[1]{0:T(128)S(6)} %copy.9.len_ref, bf16[128,512]{1,0:T(8,128)(2,1)} %att_in_ref.1), custom_call_target="tpu_custom_call" | custom-call | tf_op jit(solution)/shard_map/pallas_call | solution.py:219
  130.3 14.3 %all_to_all.21.gx_ref = bf16[16,128,128]{2,1,0:T(8,128)(2,1)} all-to-all(bf16[16,128,128]{2,1,0:T(8,128)(2,1)} %shard_map.86), channel_id=1, replica_groups=mesh['row'=8,'col'=16] {'col'}, dimensions={0} | all-to-all | bytes 1048576 | tf_op jit(solution)/shard_map/all_to_all | solution.py:310
  144.6 5.3 %shard_map.87 = f32[64,32,128]{2,1,0:T(8,128)} custom-call(bf16[16,128,128]{2,1,0:T(8,128)(2,1)} %all_to_all.21.gx_ref, f32[16,128,128]{2,1,0:T(8,128)} %get-tuple-element.14.mid_ref, bf16[128,128]{1,0:T(8,128)(2,1)} %att_out_ref.1), custom_call_target="tpu_custom_call" | custom-call | tf_op jit(solution)/shard_map/pallas_call | solution.py:219
Async XLA Ops:
  10.2 40.9 %copy-start.2 = (bf16[128,4]{0,1:T(4,128)(2,1)S(1)}, bf16[128,4]{0,1:T(4,128)(2,1)}, u32[]{:S(2)}) copy-start(bf16[128,4]{0,1:T(4,128)(2,1)} %param.14) | copy-start | bytes 3076
  44.5 18.6 %all-to-all-start.1 = ((bf16[128,16,128]{2,1,0:T(8,128)(2,1)}), bf16[128,16,128]{2,1,0:T(8,128)(2,1)S(1)}, u32[]{:S(2)}, u32[]{:S(2)}) async-start(bf16[128,16,128]{2,1,0:T(8,128)(2,1)} %shard_map.83), calls=%async_computation.1 | async-start | bytes 1048576 | tf_op jit(solution)/shard_map/all_to_all | solution.py:280
  63.1 0.8 copy-start
  76.4 32.5 %all-to-all-start.2 = ((bf16[16,128,128]{2,1,0:T(8,128)(2,1)}), bf16[16,128,128]{2,1,0:T(8,128)(2,1)S(1)}, u32[]{:S(2)}, u32[]{:S(2)}) async-start(bf16[16,128,128]{2,1,0:T(8,128)(2,1)} %get-tuple-element.12), calls=%async_computation.2 | async-start | bytes 1048576 | tf_op jit(solution)/shard_map/all_to_all | solution.py:287
  108.9 0.8 copy-start.1

commit v2 on v1

v2 whole, which is shorter than its diff:
```python
import jax
import jax.numpy as jnp
from jax import lax
from jax.experimental import pallas as pl
from jax.experimental.pallas import tpu as pltpu
from jax.sharding import PartitionSpec as P

MESH = pl.DeviceIdType.MESH
F32 = jnp.float32
BF16 = jnp.bfloat16
NT = (((1,), (1,)), ((), ()))
TN = (((0,), (0,)), ((), ()))
NN = (((1,), (0,)), ((), ()))


def dot(a, b, dims=NN):
    return lax.dot_general(a, b, dims, preferred_element_type=F32)


def norm_last(x):
    c = x - jnp.mean(x, axis=-1, keepdims=True)
    return c * lax.rsqrt(jnp.mean(c * c, axis=-1, keepdims=True) + 1e-5)


def turned(w):
    return w.astype(F32).T.astype(BF16)


def swap16():
    p = lax.broadcasted_iota(jnp.int32, (256, 256), 0)
    q = lax.broadcasted_iota(jnp.int32, (256, 256), 1)
    return (q == (p % 16) * 16 + p // 16).astype(F32).astype(BF16)


def block_turn(tiles):
    return [
        jnp.concatenate([t[:, 32 * b : 32 * b + 32] for t in tiles], axis=1) for b in range(4)
    ]


def tile_of(x_ref, s):
    return jnp.concatenate([x_ref[16 * b + s] for b in range(4)], axis=0)


def rows16(start):
    return pl.ds(pl.multiple_of(16 * start, 16), 16)


def loop(low, high, body, unroll=1):
    def step(n, carry):
        body(n)
        return carry

    lax.fori_loop(low, high, step, 0, unroll=unroll)


def push(src, dst, send_sem, recv_sem, row, col):
    pltpu.make_async_remote_copy(src, dst, send_sem, recv_sem, (row, col), MESH).start()


def take(ref, sem):
    pltpu.make_async_copy(ref, ref, sem).wait()


def kernel(
    x_ref, len_ref, tri_in_ref, tri_gate_ref, tri_out_ref, bias_ref, att_in_ref, att_out_ref, y_ref,
    wt, wvt, wgt, y, e, rx, n, lm, rm, po, px, gate, np_, yb, mid, nm, nx, bm, bx,
    qs, ks, vt, gt, bias, tile, go, gx,
    edge_send, edge_recv, prod_send, prod_recv, norm_send, norm_recv,
    near_send, near, far_send, far, back_send, back_recv,
):
    row, col = lax.axis_index("row"), lax.axis_index("col")
    me = 16 * row + col
    chip, core = col // 2, col % 2
    mate = col + 1 - 2 * core
    bar = pltpu.get_barrier_semaphore()

    def greet(k):
        t = lax.rem(me + k, 128)
        pl.semaphore_signal(bar, inc=1, device_id=(t // 16, t % 16), device_id_type=MESH)

    loop(1, 128, greet)

    wt[...] = turned(tri_in_ref[...])
    perm = swap16()
    lane128 = lax.broadcasted_iota(jnp.int32, (1, 128), 1)
    length = len_ref[0]
    keep_k = (32 * col + lane128 % 32) < length
    for side in range(2):

        def edge(s):
            if side == 0:
                nb = norm_last(tile_of(x_ref, s)).astype(BF16)
                n[s] = nb
            else:
                nb = n[s]
            pt = dot(wt[256 * side : 256 * side + 256], nb, NT)
            w = jnp.where(keep_k & ((64 * row + (lane128 // 32) * 16 + s) < length), 1.0, 0.0)
            v = (jax.nn.sigmoid(pt[:128]) * pt[128:] * w).astype(BF16)
            for g in range(8):
                at = slice(128 * (g % 2), 128 * (g % 2) + 128)
                y[g // 2, rows16(s), at] = v[16 * g : 16 * g + 16]

        loop(0, 16, edge, 4)

        def order(g):
            z = dot(perm, y[g]).astype(BF16)
            e[side, rows16(2 * g)] = z[:, :128].reshape(16, 16, 128)
            e[side, rows16(2 * g + 1)] = z[:, 128:].reshape(16, 16, 128)

        loop(0, 4, order, 4)
        if side == 0:
            pl.semaphore_wait(bar, 127)

        def send_edge(k):
            t = lax.rem(me + k, 128)
            push(
                e.at[side, t], rx.at[side, me], edge_send.at[side], edge_recv.at[side], t // 16, t % 16
            )

        loop(1, 128, send_edge)
        rx[side, me] = e[side, me]

    def make_gate(s):
        gate[s] = jax.nn.sigmoid(dot(n[s], tri_gate_ref[...]))

    loop(0, 16, make_gate, 4)
    wvt[...] = turned(att_in_ref[:, 256:384])
    wgt[...] = turned(att_in_ref[:, 384:512])

    for side, m in ((0, lm), (1, rm)):
        take(rx.at[side, pl.ds(0, 127)], edge_recv.at[side])

        def gather(r):
            for cg in range(4):
                tiles = [rx[side, 16 * r + 4 * cg + c] for c in range(4)]
                for b, t in enumerate(block_turn(tiles)):
                    m[rows16(4 * r + b), 128 * cg : 128 * cg + 128] = t

        loop(0, 8, gather, 4)

    def product(o):
        r = lax.rem(row + o, 8)
        p = dot(lm[pl.ds(pl.multiple_of(64 * r, 64), 64), :], rm[...], NT).astype(BF16)
        for cg in range(4):
            tiles = [p[16 * b : 16 * b + 16, 128 * cg : 128 * cg + 128] for b in range(4)]
            for c, t in enumerate(block_turn(tiles)):
                po[16 * r + 4 * cg + c] = t

        def send_product(k):
            c = lax.rem(col + k, 16)
            push(po.at[16 * r + c], px.at[me], prod_send, prod_recv, r, c)

        loop(jnp.where(o == 0, 1, 0), 16, send_product)

    loop(0, 8, product)
    px[me] = po[me]
    take(px.at[pl.ds(0, 127)], prod_recv)

    zero = jnp.zeros((16, 128), F32)
    total = lax.fori_loop(0, 128, lambda c, a: a + px[c].astype(F32), zero, unroll=16)
    mean = total * (1.0 / 128)

    def square(c, a):
        d = px[c].astype(F32) - mean
        return a + d * d

    scale = lax.rsqrt(lax.fori_loop(0, 128, square, zero, unroll=16) * (1.0 / 128) + 1e-5)

    def normed(g):
        z = ((px[rows16(g)].astype(F32) - mean[None]) * scale[None]).astype(BF16)
        z = dot(perm, z.reshape(256, 128)).astype(BF16)
        np_[:, rows16(g), :] = z.reshape(16, 16, 128)

    loop(0, 8, normed, 4)
    wb = bias_ref[...]

    def middle(q):
        for s in [4 * q + k for k in range(4)]:
            m = tile_of(x_ref, s) + gate[s] * dot(np_[s], tri_out_ref[...], TN)
            mid[s] = m
            nb = norm_last(m).astype(BF16)
            nm[s] = nb
            yb[pl.ds(s, 8, stride=16), :] = dot(wb, nb, NT)
        for k in range(4):
            s = 4 * q + k

            @pl.when(s != col)
            def _():
                push(nm.at[s], nx.at[col], norm_send, norm_recv, row, s)

    loop(0, 4, middle)
    nx[col] = nm[col]
    yt = yb[...].T
    bm[...] = jnp.concatenate([yt[32 * b : 32 * b + 32, :64] for b in range(4)], axis=1).astype(BF16)
    mine = 64 * core + 8 * row + chip

    def send_bias(o):
        to = lax.rem(row - o + 8, 8)

        def one(k):
            r = lax.rem(row + k, 8)

            @pl.when((k > 0) | (to != chip))
            def _():
                push(bm, bx.at[mine], near_send, near.at[o], r, 2 * to + core)

            @pl.when(o == 0)
            def _():
                push(bm, bx.at[mine], near_send, near.at[o], r, 2 * to + 1 - core)

        loop(0, 8, one)

    loop(0, 8, send_bias)
    bx[mine] = bm[...]

    kk = lax.broadcasted_iota(jnp.int32, (512, 256), 0)
    mask = jnp.where(kk < length, 0.0, -1e9).astype(F32).reshape(8, 2, 32, 256)
    own_step = lax.rem(row - chip + 8, 8)
    take(nx.at[pl.ds(0, 15)], norm_recv)

    def project(c):
        nb = nx[c]
        qk = dot(nb, att_in_ref[:, :256])
        qs[c] = (qk[:, :128] * 32 ** (-0.5)).astype(BF16)
        ks[c] = qk[:, 128:].astype(BF16)
        gt[c] = jax.nn.sigmoid(dot(wgt[...], nb, NT))

    loop(0, 16, project, 4)
    for b in range(4):
        vt[b, :128] = dot(wvt[...], nx[:, 32 * b : 32 * b + 32, :].reshape(512, 128), NT).astype(BF16)
        vt[b, 128:] = jnp.ones((16, 512), BF16)
    tile[...] = jnp.zeros((2, 128, 128), F32)

    def await_near(o, count):
        @pl.when(o == own_step)
        def _():
            take(bx.at[pl.ds(0, count - 1)], near.at[o])

        @pl.when(o != own_step)
        def _():
            take(bx.at[pl.ds(0, count)], near.at[o])

    def block(o):
        r = lax.rem(chip + o, 8)

        @pl.when(o == 0)
        def _():
            await_near(0, 16)

        @pl.when(o > 0)
        def _():
            take(bx.at[pl.ds(0, 8)], far.at[o])

        for k in range(2):
            got = bx[pl.ds(pl.multiple_of(64 * k + 8 * r, 8), 8)].astype(F32)
            bias[:, k] = got + mask[:, k]
        for b in range(4):
            if b == 2:

                @pl.when(o < 7)
                def _():
                    await_near(o + 1, 8)
                    ahead = bx.at[pl.ds(64 * core + 8 * lax.rem(r + 1, 8), 8)]
                    push(ahead, ahead, far_send, far.at[o + 1], row, mate)

            q = qs[pl.ds(2 * r, 2), 32 * b : 32 * b + 32, :].reshape(4, 1, 16, 128)
            hd = lax.broadcasted_iota(jnp.int32, (4, 4, 16, 128), 1)
            ln = lax.broadcasted_iota(jnp.int32, (4, 4, 16, 128), 3)
            qm = jnp.where(
                hd == ln // 32, jnp.broadcast_to(q, (4, 4, 16, 128)).astype(F32), 0.0
            ).astype(BF16)
            keys = ks[:, 32 * b : 32 * b + 32, :].reshape(512, 128)
            st = dot(keys, qm.reshape(256, 128), NT) + bias[...].reshape(512, 256)
            p = jnp.exp(st - jnp.max(st, axis=0, keepdims=True)).astype(BF16)
            ot = dot(vt[b], p)
            ot = ot[:128] / ot[128:129]
            for h in range(4):
                part = ot[32 * h : 32 * h + 32]
                for j in range(4):
                    at = 64 * (j % 2) + 16 * h
                    to = 32 * b + 16 * (j % 2)
                    moved = part[:, 128 * (j // 2) : 128 * (j // 2) + 128]
                    if (to - at) % 128:
                        moved = pltpu.roll(moved, (to - at) % 128, 1)
                    here = (lane128 >= to) & (lane128 < to + 16)
                    rows = slice(32 * h, 32 * h + 32)
                    tile[j // 2, rows] = jnp.where(here, moved, tile[j // 2, rows])
        for k in range(2):
            c = 2 * r + k
            go[c] = (tile[k] * gt[c]).astype(BF16)
        for k in range(2):
            c = 2 * r + k

            @pl.when(c != col)
            def _():
                push(go.at[c], gx.at[col], back_send, back_recv, row, c)

    loop(0, 8, block)
    gx[col] = go[col]
    take(gx.at[pl.ds(0, 15)], back_recv)

    def final(s):
        out = mid[s] + dot(gx[s], att_out_ref[...], TN)
        for b in range(4):
            y_ref[16 * b + s] = out[32 * b : 32 * b + 32]

    loop(0, 16, final, 4)
    for side in range(2):
        take(e.at[side, pl.ds(0, 127)], edge_send.at[side])
    take(px.at[pl.ds(0, 127)], prod_send)
    take(nx.at[pl.ds(0, 15)], norm_send)
    take(bx.at[pl.ds(0, 71)], near_send)
    take(bx.at[pl.ds(0, 56)], far_send)
    take(gx.at[pl.ds(0, 15)], back_send)


SCRATCH = [
    ((512, 128), BF16),
    ((128, 128), BF16),
    ((128, 128), BF16),
    ((4, 256, 256), BF16),
    ((2, 128, 16, 128), BF16),
    ((2, 128, 16, 128), BF16),
    ((16, 128, 128), BF16),
    ((512, 512), BF16),
    ((512, 512), BF16),
    ((128, 16, 128), BF16),
    ((128, 16, 128), BF16),
    ((16, 128, 128), F32),
    ((16, 128, 128), BF16),
    ((128, 128), F32),
    ((16, 128, 128), F32),
    ((16, 128, 128), BF16),
    ((16, 128, 128), BF16),
    ((32, 256), BF16),
    ((128, 32, 256), BF16),
    ((16, 128, 128), BF16),
    ((16, 128, 128), BF16),
    ((4, 144, 512), BF16),
    ((16, 128, 128), F32),
    ((8, 2, 32, 256), F32),
    ((2, 128, 128), F32),
    ((16, 128, 128), BF16),
    ((16, 128, 128), BF16),
]
SEMAPHORES = [(2,), (2,), (), (), (), (), (), (8,), (), (8,), (), ()]


def per_device(pair, valid_length, tri_in, tri_gate, tri_out, att_in, att_bias, att_out):
    bias8 = jnp.pad(att_bias.T, ((0, 4), (0, 0)))
    vmem = pl.BlockSpec(memory_space=pltpu.VMEM)
    smem = pl.BlockSpec(memory_space=pltpu.SMEM)
    return pl.pallas_call(
        kernel,
        out_shape=jax.ShapeDtypeStruct((64, 32, 128), F32),
        in_specs=[vmem, smem] + [vmem] * 6,
        out_specs=vmem,
        scratch_shapes=[pltpu.VMEM(*s) for s in SCRATCH]
        + [pltpu.SemaphoreType.DMA(s) for s in SEMAPHORES],
        compiler_params=pltpu.CompilerParams(
            collective_id=0, has_side_effects=True, vmem_limit_bytes=56 * 1024 * 1024
        ),
    )(pair, valid_length, tri_in, tri_gate, tri_out, bias8, att_in, att_out)


def solution(mesh):
    placed = (P("row", "col", None), P(), P(), P(), P(), P(), P(), P())
    return jax.shard_map(
        per_device, mesh=mesh, in_specs=placed, out_specs=P("row", "col", None), check_vma=False
    )
```

time: 152 us -> 92.9 us (0.61)
  the two profiles are of different devices: /device:TPU:33 before, /device:TPU:1 now
where the time goes in v2:
time: 92.9 us; the launch traced here: 92.7 us
  Pallas kernels  88.5 us (95%)
  local copies, waits for them, and re-layouts  3.52 us (4%)
    pallas_call x1, Pallas kernels, per_device(): pl.pallas_call(kernel, out_shape=jax.ShapeDtypeStruct((64, 32, 128), F32)...  88.5 us
    unnamed x3, local copies, waits for them, and re-layouts  2.94 us

profile of v2, /device:TPU:1, one launch (start us, length us, event | category | flops | bytes accessed | tf_op | source)
XLA Modules:
  0.0 92.7 jit_solution(9286758789775933214)
XLA Ops:
  0.7 0.0 copy-start
  0.7 0.7 copy-done
  1.3 0.6 pad.4.bias_ref
  1.9 88.5 %shard_map.82 = f32[64,32,128]{2,1,0:T(8,128)} custom-call(f32[64,32,128]{2,1,0:T(8,128)} %x_ref.1, s32[1]{0:T(128)S(6)} %copy.10.len_ref, bf16[128,512]{1,0:T(8,128)(2,1)} %tri_in_ref.1, bf16[128,128]{1,0:T(8,128)(2,1)} %tri_gate_ref.1, bf16[128,128]{1,0:T(8,128)(2,1)} %tri_out_ref.1, bf16[8,128]{1,0:T(8,128)(2,1)} %pad.4.bias_ref, ...), custom_call_target="tpu_custom_call" | custom-call | tf_op jit(solution)/shard_map/pallas_call | solution.py:354
  90.4 2.3 %copy.11 = f32[64,32,128]{2,1,0:T(8,128)} copy(f32[64,32,128]{2,1,0:T(8,128)} %shard_map.82) | data formatting | bytes 2097152
Async XLA Ops:
  0.7 0.7 copy-start

commit v3 on v2

--- a/solution.py
+++ b/solution.py
@@ -63,97 +63,109 @@
 
 
 def kernel(
-    x_ref, len_ref, tri_in_ref, tri_gate_ref, tri_out_ref, bias_ref, att_in_ref, att_out_ref, y_ref,
-    wt, wvt, wgt, y, e, rx, n, lm, rm, po, px, gate, np_, yb, mid, nm, nx, bm, bx,
-    qs, ks, vt, gt, bias, tile, go, gx,
-    edge_send, edge_recv, prod_send, prod_recv, norm_send, norm_recv,
-    near_send, near, far_send, far, back_send, back_recv,
+    x_hbm, len_ref, tri_in_ref, tri_gate_ref, tri_out_ref, bias_ref, att_in_ref, mid, gx,
+    x_ref, wt, wvt, wgt, y, e, rx, n, lm, rm, po, px, gate, np_, yb, nm, nx, bm, bx,
+    qs, ks, vt, gt, bias, tile, go,
+    load, right_send, right_recv, left_send, left_recv, prod_send, prod_recv, norm_send, norm_recv,
+    line_send, line, near_send, near, far_send, far, back_send, back_recv,
 ):
     row, col = lax.axis_index("row"), lax.axis_index("col")
     me = 16 * row + col
     chip, core = col // 2, col % 2
+    z_lo, x_at = chip // 4, chip % 4
     mate = col + 1 - 2 * core
     bar = pltpu.get_barrier_semaphore()
-
-    def greet(k):
-        t = lax.rem(me + k, 128)
-        pl.semaphore_signal(bar, inc=1, device_id=(t // 16, t % 16), device_id_type=MESH)
-
-    loop(1, 128, greet)
-
+    fetch = pltpu.make_async_copy(x_hbm, x_ref, load)
+    fetch.start()
+
+    def greet(r, first=0):
+        for k in range(first, 16):
+            c = lax.rem(col + k, 16)
+            pl.semaphore_signal(bar, inc=1, device_id=(r, c), device_id_type=MESH)
+
+    greet(row, 1)
+    loop(1, 8, lambda a: greet(lax.rem(row + a, 8)))
     wt[...] = turned(tri_in_ref[...])
     perm = swap16()
     lane128 = lax.broadcasted_iota(jnp.int32, (1, 128), 1)
     length = len_ref[0]
     keep_k = (32 * col + lane128 % 32) < length
-    for side in range(2):
-
-        def edge(s):
-            if side == 0:
-                nb = norm_last(tile_of(x_ref, s)).astype(BF16)
-                n[s] = nb
-            else:
-                nb = n[s]
-            pt = dot(wt[256 * side : 256 * side + 256], nb, NT)
-            w = jnp.where(keep_k & ((64 * row + (lane128 // 32) * 16 + s) < length), 1.0, 0.0)
-            v = (jax.nn.sigmoid(pt[:128]) * pt[128:] * w).astype(BF16)
-            for g in range(8):
-                at = slice(128 * (g % 2), 128 * (g % 2) + 128)
-                y[g // 2, rows16(s), at] = v[16 * g : 16 * g + 16]
-
-        loop(0, 16, edge, 4)
-
-        def order(g):
+    fetch.wait()
+
+    def edge(side, s, nb):
+        pt = dot(wt[256 * side : 256 * side + 256], nb, NT)
+        w = jnp.where(keep_k & ((64 * row + (lane128 // 32) * 16 + s) < length), 1.0, 0.0)
+        v = (jax.nn.sigmoid(pt[:128]) * pt[128:] * w).astype(BF16)
+        for g in range(8):
+            at = slice(128 * (g % 2), 128 * (g % 2) + 128)
+            y[g // 2, rows16(s), at] = v[16 * g : 16 * g + 16]
+
+    def order(side):
+        for g in range(4):
             z = dot(perm, y[g]).astype(BF16)
-            e[side, rows16(2 * g)] = z[:, :128].reshape(16, 16, 128)
-            e[side, rows16(2 * g + 1)] = z[:, 128:].reshape(16, 16, 128)
-
-        loop(0, 4, order, 4)
-        if side == 0:
-            pl.semaphore_wait(bar, 127)
-
-        def send_edge(k):
-            t = lax.rem(me + k, 128)
-            push(
-                e.at[side, t], rx.at[side, me], edge_send.at[side], edge_recv.at[side], t // 16, t % 16
-            )
-
-        loop(1, 128, send_edge)
-        rx[side, me] = e[side, me]
-
-    def make_gate(s):
-        gate[s] = jax.nn.sigmoid(dot(n[s], tri_gate_ref[...]))
-
-    loop(0, 16, make_gate, 4)
+            e[side, 32 * g : 32 * g + 16] = z[:, :128].reshape(16, 16, 128)
+            e[side, 32 * g + 16 : 32 * g + 32] = z[:, 128:].reshape(16, 16, 128)
+
+    def first_edge(s):
+        nb = norm_last(tile_of(x_ref, s)).astype(BF16)
+        n[s] = nb
+        edge(1, s, nb)
+
+    def send_right(a):
+        r = lax.rem(row + a, 8)
+        for k in range(1 if a == 0 else 0, 16):
+            c = lax.rem(col + k, 16)
+            push(e.at[1, 16 * r + c], rx.at[1, me], right_send, right_recv, r, c)
+
+    def send_left(a):
+        r = lax.rem(row + 8 - a, 8)
+        for k in range(1 if a == 0 else 0, 16):
+            c = lax.rem(col + k, 16)
+            push(e.at[0, 16 * r + c], rx.at[0, me], left_send, left_recv.at[a], r, c)
+
+    loop(0, 16, first_edge, 4)
+    order(1)
+    pl.semaphore_wait(bar, 127)
+    for q in range(4):
+        send_right(2 * q)
+        send_right(2 * q + 1)
+        for s in range(4 * q, 4 * q + 4):
+            edge(0, s, n[s])
+    rx[1, me] = e[1, me]
+    order(0)
+    for q in range(4):
+        send_left(2 * q)
+        send_left(2 * q + 1)
+        for s in range(4 * q, 4 * q + 4):
+            gate[s] = jax.nn.sigmoid(dot(n[s], tri_gate_ref[...]))
+    rx[0, me] = e[0, me]
     wvt[...] = turned(att_in_ref[:, 256:384])
     wgt[...] = turned(att_in_ref[:, 384:512])
 
-    for side, m in ((0, lm), (1, rm)):
-        take(rx.at[side, pl.ds(0, 127)], edge_recv.at[side])
-
-        def gather(r):
-            for cg in range(4):
-                tiles = [rx[side, 16 * r + 4 * cg + c] for c in range(4)]
-                for b, t in enumerate(block_turn(tiles)):
-                    m[rows16(4 * r + b), 128 * cg : 128 * cg + 128] = t
-
-        loop(0, 8, gather, 4)
-
-    def product(o):
+    def assemble(side, r, m, at):
+        for cg in range(4):
+            tiles = [rx[side, 16 * r + 4 * cg + c] for c in range(4)]
+            for b, t in enumerate(block_turn(tiles)):
+                m[rows16(at + b), 128 * cg : 128 * cg + 128] = t
+
+    take(rx.at[1, pl.ds(0, 127)], right_recv)
+    loop(0, 8, lambda r: assemble(1, r, rm, 4 * r), 4)
+
+    def product(o, first=0):
         r = lax.rem(row + o, 8)
-        p = dot(lm[pl.ds(pl.multiple_of(64 * r, 64), 64), :], rm[...], NT).astype(BF16)
+        take(rx.at[0, pl.ds(0, 16 - first)], left_recv.at[o])
+        assemble(0, r, lm, 0)
+        p = dot(lm[...], rm[...], NT).astype(BF16)
         for cg in range(4):
             tiles = [p[16 * b : 16 * b + 16, 128 * cg : 128 * cg + 128] for b in range(4)]
             for c, t in enumerate(block_turn(tiles)):
                 po[16 * r + 4 * cg + c] = t
-
-        def send_product(k):
+        for k in range(first, 16):
             c = lax.rem(col + k, 16)
             push(po.at[16 * r + c], px.at[me], prod_send, prod_recv, r, c)
 
-        loop(jnp.where(o == 0, 1, 0), 16, send_product)
-
-    loop(0, 8, product)
+    product(0, 1)
+    loop(1, 8, product)
     px[me] = po[me]
     take(px.at[pl.ds(0, 127)], prod_recv)
 
@@ -174,6 +186,11 @@
 
     loop(0, 8, normed, 4)
     wb = bias_ref[...]
+
+    def send_norm(s):
+        @pl.when(s != col)
+        def _():
+            push(nm.at[s], nx.at[col], norm_send, norm_recv, row, s)
 
     def middle(q):
         for s in [4 * q + k for k in range(4)]:
@@ -181,42 +198,45 @@
             mid[s] = m
             nb = norm_last(m).astype(BF16)
             nm[s] = nb
-            yb[pl.ds(s, 8, stride=16), :] = dot(wb, nb, NT)
-        for k in range(4):
-            s = 4 * q + k
-
-            @pl.when(s != col)
+            yb[pl.ds(s, 4, stride=16), :] = dot(wb, nb, NT)
+
+        @pl.when(q < 2)
+        def _():
+            for k in range(4):
+                send_norm(4 * q + k)
+
+    loop(0, 4, middle)
+    yt = yb[...].T
+    bm[...] = jnp.concatenate([yt[32 * b : 32 * b + 32] for b in range(4)], axis=1).astype(BF16)
+    line_of = 64 * core + 8 * row + 4 * z_lo
+    mine = line_of + x_at
+    for k in range(1, 4):
+        c = 8 * z_lo + 2 * lax.rem(x_at + k, 4) + core
+        push(bm, bx.at[mine], line_send, line, row, c)
+    loop(8, 16, send_norm)
+    nx[col] = nm[col]
+    bx[mine] = bm[...]
+    take(bx.at[pl.ds(0, 3)], line)
+    own_step = lax.rem(8 - chip, 8)
+
+    def send_bias(o):
+        group = bx.at[pl.ds(line_of, 4)]
+        for z in range(2):
+            r = lax.rem(row - x_at - 4 * z - o + 16, 8)
+            c = 8 * z + 2 * x_at
+
+            @pl.when((r != row) | (z_lo != z))
             def _():
-                push(nm.at[s], nx.at[col], norm_send, norm_recv, row, s)
-
-    loop(0, 4, middle)
-    nx[col] = nm[col]
-    yt = yb[...].T
-    bm[...] = jnp.concatenate([yt[32 * b : 32 * b + 32, :64] for b in range(4)], axis=1).astype(BF16)
-    mine = 64 * core + 8 * row + chip
-
-    def send_bias(o):
-        to = lax.rem(row - o + 8, 8)
-
-        def one(k):
-            r = lax.rem(row + k, 8)
-
-            @pl.when((k > 0) | (to != chip))
-            def _():
-                push(bm, bx.at[mine], near_send, near.at[o], r, 2 * to + core)
+                push(group, group, near_send, near.at[o], r, c + core)
 
             @pl.when(o == 0)
             def _():
-                push(bm, bx.at[mine], near_send, near.at[o], r, 2 * to + 1 - core)
-
-        loop(0, 8, one)
+                push(group, group, near_send, near.at[o], r, c + 1 - core)
 
     loop(0, 8, send_bias)
-    bx[mine] = bm[...]
 
     kk = lax.broadcasted_iota(jnp.int32, (512, 256), 0)
     mask = jnp.where(kk < length, 0.0, -1e9).astype(F32).reshape(8, 2, 32, 256)
-    own_step = lax.rem(row - chip + 8, 8)
     take(nx.at[pl.ds(0, 15)], norm_recv)
 
     def project(c):
@@ -235,14 +255,14 @@
     def await_near(o, count):
         @pl.when(o == own_step)
         def _():
-            take(bx.at[pl.ds(0, count - 1)], near.at[o])
+            take(bx.at[pl.ds(0, count - 4)], near.at[o])
 
         @pl.when(o != own_step)
         def _():
             take(bx.at[pl.ds(0, count)], near.at[o])
 
     def block(o):
-        r = lax.rem(chip + o, 8)
+        r = lax.rem(chip + row + o, 8)
 
         @pl.when(o == 0)
         def _():
@@ -298,24 +318,26 @@
 
     loop(0, 8, block)
     gx[col] = go[col]
-    take(gx.at[pl.ds(0, 15)], back_recv)
-
-    def final(s):
-        out = mid[s] + dot(gx[s], att_out_ref[...], TN)
-        for b in range(4):
-            y_ref[16 * b + s] = out[32 * b : 32 * b + 32]
-
-    loop(0, 16, final, 4)
-    for side in range(2):
-        take(e.at[side, pl.ds(0, 127)], edge_send.at[side])
+    take(rx.at[0, pl.ds(0, 127)], right_send)
+    take(rx.at[0, pl.ds(0, 127)], left_send)
     take(px.at[pl.ds(0, 127)], prod_send)
     take(nx.at[pl.ds(0, 15)], norm_send)
-    take(bx.at[pl.ds(0, 71)], near_send)
+    take(bx.at[pl.ds(0, 3)], line_send)
+    take(bx.at[pl.ds(0, 68)], near_send)
     take(bx.at[pl.ds(0, 56)], far_send)
     take(gx.at[pl.ds(0, 15)], back_send)
+    take(gx.at[pl.ds(0, 15)], back_recv)
+
+
+def final(gx_ref, mid_ref, att_out_ref, y_ref):
+    for s in range(4):
+        out = mid_ref[s] + dot(gx_ref[s], att_out_ref[...], TN)
+        for b in range(4):
+            y_ref[b, s] = out[32 * b : 32 * b + 32]
 
 
 SCRATCH = [
+    ((64, 32, 128), F32),
     ((512, 128), BF16),
     ((128, 128), BF16),
     ((128, 128), BF16),
@@ -323,14 +345,13 @@
     ((2, 128, 16, 128), BF16),
     ((2, 128, 16, 128), BF16),
     ((16, 128, 128), BF16),
-    ((512, 512), BF16),
+    ((64, 512), BF16),
     ((512, 512), BF16),
     ((128, 16, 128), BF16),
     ((128, 16, 128), BF16),
     ((16, 128, 128), F32),
     ((16, 128, 128), BF16),
-    ((128, 128), F32),
-    ((16, 128, 128), F32),
+    ((64, 128), F32),
     ((16, 128, 128), BF16),
     ((16, 128, 128), BF16),
     ((32, 256), BF16),
@@ -342,26 +363,36 @@
     ((8, 2, 32, 256), F32),
     ((2, 128, 128), F32),
     ((16, 128, 128), BF16),
-    ((16, 128, 128), BF16),
 ]
-SEMAPHORES = [(2,), (2,), (), (), (), (), (), (8,), (), (8,), (), ()]
+SEMAPHORES = [(), (), (), (), (8,), (), (), (), (), (), (), (), (8,), (), (8,), (), ()]
 
 
 def per_device(pair, valid_length, tri_in, tri_gate, tri_out, att_in, att_bias, att_out):
-    bias8 = jnp.pad(att_bias.T, ((0, 4), (0, 0)))
     vmem = pl.BlockSpec(memory_space=pltpu.VMEM)
     smem = pl.BlockSpec(memory_space=pltpu.SMEM)
-    return pl.pallas_call(
+    middle, back = pl.pallas_call(
         kernel,
-        out_shape=jax.ShapeDtypeStruct((64, 32, 128), F32),
-        in_specs=[vmem, smem] + [vmem] * 6,
-        out_specs=vmem,
+        out_shape=[
+            jax.ShapeDtypeStruct((16, 128, 128), F32),
+            jax.ShapeDtypeStruct((16, 128, 128), BF16),
+        ],
+        in_specs=[pl.BlockSpec(memory_space=pl.ANY), smem] + [vmem] * 5,
+        out_specs=[vmem, vmem],
         scratch_shapes=[pltpu.VMEM(*s) for s in SCRATCH]
         + [pltpu.SemaphoreType.DMA(s) for s in SEMAPHORES],
         compiler_params=pltpu.CompilerParams(
             collective_id=0, has_side_effects=True, vmem_limit_bytes=56 * 1024 * 1024
         ),
-    )(pair, valid_length, tri_in, tri_gate, tri_out, bias8, att_in, att_out)
+    )(pair, valid_length, tri_in, tri_gate, tri_out, att_bias.T, att_in)
+    tiles = pl.BlockSpec((4, 128, 128), lambda s: (s, 0, 0))
+    out = pl.pallas_call(
+        final,
+        grid=(4,),
+        out_shape=jax.ShapeDtypeStruct((4, 16, 32, 128), F32),
+        in_specs=[tiles, tiles, pl.BlockSpec((128, 128), lambda s: (0, 0))],
+        out_specs=pl.BlockSpec((4, 4, 32, 128), lambda s: (0, s, 0, 0)),
+    )(back, middle, att_out)
+    return out.reshape(64, 32, 128)
 
 
 def solution(mesh):

time: 92.9 us -> 89.1 us (0.959)
  the two profiles are of different devices: /device:TPU:1 before, /device:TPU:13 now
where the time goes in v3:
time: 89.1 us; the launch traced here: 88.8 us
  Pallas kernels  88.2 us (99%)
    pallas_call x1, Pallas kernels, per_device(): pl.pallas_call(kernel, out_shape=[jax.ShapeDtypeStruct((16, 128, 128), F3...  84.3 us
    pallas_call x1, Pallas kernels, per_device(): pl.pallas_call(final, grid=(4,), out_shape=jax.ShapeDtypeStruct((4, 16, 3...  3.92 us

profile of v3, /device:TPU:13, one launch (start us, length us, event | category | flops | bytes accessed | tf_op | source)
XLA Modules:
  0.0 88.8 jit_solution(5483393284424558275)
XLA Ops:
  0.7 84.3 %shard_map.82 = (f32[16,128,128]{2,1,0:T(8,128)}, bf16[16,128,128]{2,1,0:T(8,128)(2,1)}) custom-call(f32[64,32,128]{2,1,0:T(8,128)} %x_hbm.1, s32[1]{0:T(128)S(6)} %copy.9.len_ref, bf16[128,512]{1,0:T(8,128)(2,1)} %tri_in_ref.1, bf16[128,128]{1,0:T(8,128)(2,1)} %tri_gate_ref.1, bf16[128,128]{1,0:T(8,128)(2,1)} %tri_out_ref.1, bf16[4,128]{1,0:T(4,128)(2,1)} %bitcast.2, ...), custom_call_target="tpu_custom_call" | custom-call | tf_op jit(solution)/shard_map/pallas_call | solution.py:373
  84.9 3.9 %shard_map.83 = f32[4,16,32,128]{3,2,1,0:T(8,128)} custom-call(bf16[16,128,128]{2,1,0:T(8,128)(2,1)} %get-tuple-element.7.gx_ref, f32[16,128,128]{2,1,0:T(8,128)} %get-tuple-element.8.mid_ref, bf16[128,128]{1,0:T(8,128)(2,1)} %att_out_ref.1), custom_call_target="tpu_custom_call" | custom-call | tf_op jit(solution)/shard_map/pallas_call | solution.py:388

commit v4 on v3

--- a/solution.py
+++ b/solution.py
@@ -63,16 +63,17 @@
 
 
 def kernel(
-    x_hbm, len_ref, tri_in_ref, tri_gate_ref, tri_out_ref, bias_ref, att_in_ref, mid, gx,
-    x_ref, wt, wvt, wgt, y, e, rx, n, lm, rm, po, px, gate, np_, yb, nm, nx, bm, bx,
+    x_hbm, len_ref, tri_in_ref, tri_gate_ref, tri_out_ref, bias_ref, att_in_ref, mid_hbm, gx,
+    x_ref, mid, wt, wvt, wgt, y, e, rx, n, lm, rm, po, px, gate, np_, yb, nm, nx, bm, bx,
     qs, ks, vt, gt, bias, tile, go,
     load, right_send, right_recv, left_send, left_recv, prod_send, prod_recv, norm_send, norm_recv,
-    line_send, line, near_send, near, far_send, far, back_send, back_recv,
+    line_send, line, plane_send, plane, near_send, near, far_send, far, back_send, back_recv, keep,
 ):
     row, col = lax.axis_index("row"), lax.axis_index("col")
     me = 16 * row + col
     chip, core = col // 2, col % 2
     z_lo, x_at = chip // 4, chip % 4
+    y_at, z_at = row // 2, 2 * (row % 2) + z_lo
     mate = col + 1 - 2 * core
     bar = pltpu.get_barrier_semaphore()
     fetch = pltpu.make_async_copy(x_hbm, x_ref, load)
@@ -193,7 +194,8 @@
             push(nm.at[s], nx.at[col], norm_send, norm_recv, row, s)
 
     def middle(q):
-        for s in [4 * q + k for k in range(4)]:
+        first = 4 * lax.rem(q + 2 - 2 * z_lo, 4)
+        for s in [first + k for k in range(4)]:
             m = tile_of(x_ref, s) + gate[s] * dot(np_[s], tri_out_ref[...], TN)
             mid[s] = m
             nb = norm_last(m).astype(BF16)
@@ -203,7 +205,8 @@
         @pl.when(q < 2)
         def _():
             for k in range(4):
-                send_norm(4 * q + k)
+                s = first + k
+                push(nm.at[s], nx.at[col], norm_send, norm_recv, row, s)
 
     loop(0, 4, middle)
     yt = yb[...].T
@@ -213,27 +216,35 @@
     for k in range(1, 4):
         c = 8 * z_lo + 2 * lax.rem(x_at + k, 4) + core
         push(bm, bx.at[mine], line_send, line, row, c)
-    loop(8, 16, send_norm)
+    loop(8 * z_lo, 8 * z_lo + 8, send_norm)
     nx[col] = nm[col]
     bx[mine] = bm[...]
+    saved = pltpu.make_async_copy(mid, mid_hbm, keep.at[0])
+    saved.start()
     take(bx.at[pl.ds(0, 3)], line)
-    own_step = lax.rem(8 - chip, 8)
-
-    def send_bias(o):
-        group = bx.at[pl.ds(line_of, 4)]
-        for z in range(2):
-            r = lax.rem(row - x_at - 4 * z - o + 16, 8)
-            c = 8 * z + 2 * x_at
-
-            @pl.when((r != row) | (z_lo != z))
-            def _():
-                push(group, group, near_send, near.at[o], r, c + core)
-
-            @pl.when(o == 0)
-            def _():
-                push(group, group, near_send, near.at[o], r, c + 1 - core)
-
-    loop(0, 8, send_bias)
+    group = bx.at[pl.ds(line_of, 4)]
+    for k in range(1, 4):
+        z = lax.rem(z_at + k, 4)
+        push(group, group, plane_send, plane, 2 * y_at + z // 2, 8 * (z % 2) + 2 * x_at + core)
+
+    def rows_of(o):
+        turn = 2 * (x_at % 2)
+        back = jnp.where(o < 2, 0, jnp.where(o < 4, 1 + turn, jnp.where(o < 6, 3 - turn, 2)))
+        half = lax.rem(o + x_at, 2)
+        return 2 * lax.rem(y_at - back + 4, 4) + half, 2 * back + half
+
+    def bias_rows(r):
+        return bx.at[pl.ds(64 * core + 8 * r, 8)]
+
+    take(bx.at[pl.ds(0, 12)], plane)
+    for o in range(2):
+        mine_ = bias_rows(rows_of(o)[0])
+        push(mine_, mine_, far_send, far.at[o], row, mate)
+    for k in (1, 3, 2):
+        for half in range(2):
+            mine_ = bias_rows(2 * y_at + half)
+            r = 2 * lax.rem(y_at + k, 4) + row % 2
+            push(mine_, mine_, near_send, near.at[2 * k + half], r, col)
 
     kk = lax.broadcasted_iota(jnp.int32, (512, 256), 0)
     mask = jnp.where(kk < length, 0.0, -1e9).astype(F32).reshape(8, 2, 32, 256)
@@ -252,37 +263,20 @@
         vt[b, 128:] = jnp.ones((16, 512), BF16)
     tile[...] = jnp.zeros((2, 128, 128), F32)
 
-    def await_near(o, count):
-        @pl.when(o == own_step)
-        def _():
-            take(bx.at[pl.ds(0, count - 4)], near.at[o])
-
-        @pl.when(o != own_step)
-        def _():
-            take(bx.at[pl.ds(0, count)], near.at[o])
-
     def block(o):
-        r = lax.rem(chip + row + o, 8)
-
-        @pl.when(o == 0)
-        def _():
-            await_near(0, 16)
-
-        @pl.when(o > 0)
-        def _():
-            take(bx.at[pl.ds(0, 8)], far.at[o])
-
+        r = rows_of(o)[0]
+        take(bx.at[pl.ds(0, 8)], far.at[o])
         for k in range(2):
             got = bx[pl.ds(pl.multiple_of(64 * k + 8 * r, 8), 8)].astype(F32)
             bias[:, k] = got + mask[:, k]
         for b in range(4):
             if b == 2:
 
-                @pl.when(o < 7)
+                @pl.when((o > 0) & (o < 7))
                 def _():
-                    await_near(o + 1, 8)
-                    ahead = bx.at[pl.ds(64 * core + 8 * lax.rem(r + 1, 8), 8)]
-                    push(ahead, ahead, far_send, far.at[o + 1], row, mate)
+                    later, slot = rows_of(o + 1)
+                    take(bx.at[pl.ds(0, 8)], near.at[slot])
+                    push(bias_rows(later), bias_rows(later), far_send, far.at[o + 1], row, mate)
 
             q = qs[pl.ds(2 * r, 2), 32 * b : 32 * b + 32, :].reshape(4, 1, 16, 128)
             hd = lax.broadcasted_iota(jnp.int32, (4, 4, 16, 128), 1)
@@ -317,27 +311,52 @@
                 push(go.at[c], gx.at[col], back_send, back_recv, row, c)
 
     loop(0, 8, block)
-    gx[col] = go[col]
+    own = pltpu.make_async_copy(go.at[col], gx.at[col], keep.at[1])
+    own.start()
     take(rx.at[0, pl.ds(0, 127)], right_send)
     take(rx.at[0, pl.ds(0, 127)], left_send)
     take(px.at[pl.ds(0, 127)], prod_send)
     take(nx.at[pl.ds(0, 15)], norm_send)
     take(bx.at[pl.ds(0, 3)], line_send)
-    take(bx.at[pl.ds(0, 68)], near_send)
-    take(bx.at[pl.ds(0, 56)], far_send)
-    take(gx.at[pl.ds(0, 15)], back_send)
-    take(gx.at[pl.ds(0, 15)], back_recv)
-
-
-def final(gx_ref, mid_ref, att_out_ref, y_ref):
-    for s in range(4):
-        out = mid_ref[s] + dot(gx_ref[s], att_out_ref[...], TN)
-        for b in range(4):
-            y_ref[b, s] = out[32 * b : 32 * b + 32]
+    take(bx.at[pl.ds(0, 12)], plane_send)
+    take(bx.at[pl.ds(0, 48)], near_send)
+    take(bx.at[pl.ds(0, 64)], far_send)
+    saved.wait()
+    own.wait()
+    take(go.at[pl.ds(0, 15)], back_send)
+    take(go.at[pl.ds(0, 15)], back_recv)
+
+
+def final(gx_hbm, mid_hbm, att_out_ref, y_hbm, gx, mid, y, gx_sem, mid_sem, y_sem):
+    def fetch(g):
+        at = pl.ds(4 * g, 4)
+        return (
+            pltpu.make_async_copy(gx_hbm.at[at], gx.at[at], gx_sem.at[g]),
+            pltpu.make_async_copy(mid_hbm.at[at], mid.at[at], mid_sem.at[g]),
+        )
+
+    def store(g):
+        at = pl.ds(4 * g, 4)
+        return pltpu.make_async_copy(y.at[:, at], y_hbm.at[:, at], y_sem.at[g])
+
+    for g in range(4):
+        for copy in fetch(g):
+            copy.start()
+    for g in range(4):
+        for copy in fetch(g):
+            copy.wait()
+        for s in range(4 * g, 4 * g + 4):
+            out = mid[s] + dot(gx[s], att_out_ref[...], TN)
+            for b in range(4):
+                y[b, s] = out[32 * b : 32 * b + 32]
+        store(g).start()
+    for g in range(4):
+        store(g).wait()
 
 
 SCRATCH = [
     ((64, 32, 128), F32),
+    ((16, 128, 128), F32),
     ((512, 128), BF16),
     ((128, 128), BF16),
     ((128, 128), BF16),
@@ -364,33 +383,39 @@
     ((2, 128, 128), F32),
     ((16, 128, 128), BF16),
 ]
-SEMAPHORES = [(), (), (), (), (8,), (), (), (), (), (), (), (), (8,), (), (8,), (), ()]
+SEMAPHORES = [(), (), (), (), (8,), (), (), (), (), (), (), (), (), (), (8,), (), (8,), (), (), (2,)]
 
 
 def per_device(pair, valid_length, tri_in, tri_gate, tri_out, att_in, att_bias, att_out):
     vmem = pl.BlockSpec(memory_space=pltpu.VMEM)
     smem = pl.BlockSpec(memory_space=pltpu.SMEM)
+    anywhere = pl.BlockSpec(memory_space=pl.ANY)
     middle, back = pl.pallas_call(
         kernel,
         out_shape=[
             jax.ShapeDtypeStruct((16, 128, 128), F32),
             jax.ShapeDtypeStruct((16, 128, 128), BF16),
         ],
-        in_specs=[pl.BlockSpec(memory_space=pl.ANY), smem] + [vmem] * 5,
-        out_specs=[vmem, vmem],
+        in_specs=[anywhere, smem] + [vmem] * 5,
+        out_specs=[anywhere, anywhere],
         scratch_shapes=[pltpu.VMEM(*s) for s in SCRATCH]
         + [pltpu.SemaphoreType.DMA(s) for s in SEMAPHORES],
         compiler_params=pltpu.CompilerParams(
-            collective_id=0, has_side_effects=True, vmem_limit_bytes=56 * 1024 * 1024
+            collective_id=0, has_side_effects=True, vmem_limit_bytes=60 * 1024 * 1024
         ),
     )(pair, valid_length, tri_in, tri_gate, tri_out, att_bias.T, att_in)
-    tiles = pl.BlockSpec((4, 128, 128), lambda s: (s, 0, 0))
     out = pl.pallas_call(
         final,
-        grid=(4,),
         out_shape=jax.ShapeDtypeStruct((4, 16, 32, 128), F32),
-        in_specs=[tiles, tiles, pl.BlockSpec((128, 128), lambda s: (0, 0))],
-        out_specs=pl.BlockSpec((4, 4, 32, 128), lambda s: (0, s, 0, 0)),
+        in_specs=[anywhere, anywhere, vmem],
+        out_specs=anywhere,
+        scratch_shapes=[
+            pltpu.VMEM((16, 128, 128), BF16),
+            pltpu.VMEM((16, 128, 128), F32),
+            pltpu.VMEM((4, 16, 32, 128), F32),
+        ]
+        + [pltpu.SemaphoreType.DMA((4,))] * 3,
+        compiler_params=pltpu.CompilerParams(vmem_limit_bytes=60 * 1024 * 1024),
     )(back, middle, att_out)
     return out.reshape(64, 32, 128)
 

time: 89.1 us -> 82.6 us (0.927)
  the two profiles are of different devices: /device:TPU:13 before, /device:TPU:33 now
where the time goes in v4:
time: 82.6 us; the launch traced here: 81.3 us
  Pallas kernels  80.6 us (98%)
    pallas_call x1, Pallas kernels, per_device(): pl.pallas_call(kernel, out_shape=[jax.ShapeDtypeStruct((16, 128, 128), F3...  77.1 us
    pallas_call x1, Pallas kernels, per_device(): pl.pallas_call(final, out_shape=jax.ShapeDtypeStruct((4, 16, 32, 128), F3...  3.45 us

profile of v4, /device:TPU:33, one launch (start us, length us, event | category | flops | bytes accessed | tf_op | source)
XLA Modules:
  0.0 81.3 jit_solution(7840098500385313142)
XLA Ops:
  0.7 77.1 %shard_map.82 = (f32[16,128,128]{2,1,0:T(8,128)}, bf16[16,128,128]{2,1,0:T(8,128)(2,1)}) custom-call(f32[64,32,128]{2,1,0:T(8,128)} %x_hbm.1, s32[1]{0:T(128)S(6)} %copy.9.len_ref, bf16[128,512]{1,0:T(8,128)(2,1)} %tri_in_ref.1, bf16[128,128]{1,0:T(8,128)(2,1)} %tri_gate_ref.1, bf16[128,128]{1,0:T(8,128)(2,1)} %tri_out_ref.1, bf16[4,128]{1,0:T(4,128)(2,1)} %bitcast.2, ...), custom_call_target="tpu_custom_call" | custom-call | tf_op jit(solution)/shard_map/pallas_call | solution.py:393
  77.8 3.5 %shard_map.83 = f32[4,16,32,128]{3,2,1,0:T(8,128)} custom-call(bf16[16,128,128]{2,1,0:T(8,128)(2,1)} %get-tuple-element.7.gx_hbm, f32[16,128,128]{2,1,0:T(8,128)} %get-tuple-element.8.mid_hbm, bf16[128,128]{1,0:T(8,128)(2,1)} %att_out_ref.1), custom_call_target="tpu_custom_call" | custom-call | tf_op jit(solution)/shard_map/pallas_call | solution.py:407

commit v5 on v4

--- a/solution.py
+++ b/solution.py
@@ -6,6 +6,7 @@
 from jax.sharding import PartitionSpec as P
 
 MESH = pl.DeviceIdType.MESH
+LOG2E = 1.4426950408889634
 F32 = jnp.float32
 BF16 = jnp.bfloat16
 NT = (((1,), (1,)), ((), ()))
@@ -63,9 +64,9 @@
 
 
 def kernel(
-    x_hbm, len_ref, tri_in_ref, tri_gate_ref, tri_out_ref, bias_ref, att_in_ref, mid_hbm, gx,
-    x_ref, mid, wt, wvt, wgt, y, e, rx, n, lm, rm, po, px, gate, np_, yb, nm, nx, bm, bx,
-    qs, ks, vt, gt, bias, tile, go,
+    x_hbm, len_ref, tri_in_ref, tri_gate_ref, tri_out_ref, bias_ref, att_in_ref, att_out_ref, out_hbm,
+    x_ref, gx, out, update, wt, wvt, wgt, y, e, rx, n, lm, rm, po, px, gate, np_, yb, nm, nx, bm, bx,
+    qs, ks, vt, gt, bias, scores, tile, go,
     load, right_send, right_recv, left_send, left_recv, prod_send, prod_recv, norm_send, norm_recv,
     line_send, line, plane_send, plane, near_send, near, far_send, far, back_send, back_recv, keep,
 ):
@@ -196,9 +197,9 @@
     def middle(q):
         first = 4 * lax.rem(q + 2 - 2 * z_lo, 4)
         for s in [first + k for k in range(4)]:
-            m = tile_of(x_ref, s) + gate[s] * dot(np_[s], tri_out_ref[...], TN)
-            mid[s] = m
-            nb = norm_last(m).astype(BF16)
+            u = gate[s] * dot(np_[s], tri_out_ref[...], TN)
+            update[s] = u
+            nb = norm_last(tile_of(x_ref, s) + u).astype(BF16)
             nm[s] = nb
             yb[pl.ds(s, 4, stride=16), :] = dot(wb, nb, NT)
 
@@ -219,8 +220,6 @@
     loop(8 * z_lo, 8 * z_lo + 8, send_norm)
     nx[col] = nm[col]
     bx[mine] = bm[...]
-    saved = pltpu.make_async_copy(mid, mid_hbm, keep.at[0])
-    saved.start()
     take(bx.at[pl.ds(0, 3)], line)
     group = bx.at[pl.ds(line_of, 4)]
     for k in range(1, 4):
@@ -240,8 +239,8 @@
     for o in range(2):
         mine_ = bias_rows(rows_of(o)[0])
         push(mine_, mine_, far_send, far.at[o], row, mate)
-    for k in (1, 3, 2):
-        for half in range(2):
+    for half in range(2):
+        for k in (1, 3):
             mine_ = bias_rows(2 * y_at + half)
             r = 2 * lax.rem(y_at + k, 4) + row % 2
             push(mine_, mine_, near_send, near.at[2 * k + half], r, col)
@@ -265,19 +264,26 @@
 
     def block(o):
         r = rows_of(o)[0]
+
+        @pl.when((o > 0) & (o < 7))
+        def _():
+            later, slot = rows_of(o + 1)
+            rows = bias_rows(later)
+            take(bx.at[pl.ds(0, 8)], near.at[slot])
+            push(rows, rows, far_send, far.at[o + 1], row, mate)
+            for k, half in ((1, 0), (3, 1)):
+
+                @pl.when(slot == 2 * k + half)
+                def _():
+                    to = 2 * lax.rem(y_at + k, 4) + row % 2
+                    push(rows, rows, near_send, near.at[4 + half], to, col)
+
         take(bx.at[pl.ds(0, 8)], far.at[o])
         for k in range(2):
             got = bx[pl.ds(pl.multiple_of(64 * k + 8 * r, 8), 8)].astype(F32)
-            bias[:, k] = got + mask[:, k]
-        for b in range(4):
-            if b == 2:
-
-                @pl.when((o > 0) & (o < 7))
-                def _():
-                    later, slot = rows_of(o + 1)
-                    take(bx.at[pl.ds(0, 8)], near.at[slot])
-                    push(bias_rows(later), bias_rows(later), far_send, far.at[o + 1], row, mate)
-
+            bias[:, k] = (got + mask[:, k]) * LOG2E
+
+        def score(b):
             q = qs[pl.ds(2 * r, 2), 32 * b : 32 * b + 32, :].reshape(4, 1, 16, 128)
             hd = lax.broadcasted_iota(jnp.int32, (4, 4, 16, 128), 1)
             ln = lax.broadcasted_iota(jnp.int32, (4, 4, 16, 128), 3)
@@ -285,10 +291,15 @@
                 hd == ln // 32, jnp.broadcast_to(q, (4, 4, 16, 128)).astype(F32), 0.0
             ).astype(BF16)
             keys = ks[:, 32 * b : 32 * b + 32, :].reshape(512, 128)
-            st = dot(keys, qm.reshape(256, 128), NT) + bias[...].reshape(512, 256)
-            p = jnp.exp(st - jnp.max(st, axis=0, keepdims=True)).astype(BF16)
-            ot = dot(vt[b], p)
-            ot = ot[:128] / ot[128:129]
+            st = dot(keys, qm.reshape(256, 128), NT) * LOG2E + bias[...].reshape(512, 256)
+            scores[b] = st
+            return jnp.max(st, axis=0, keepdims=True)
+
+        top = score(0)
+        for b in range(4):
+            later_top = score(b + 1) if b < 3 else None
+            ot = dot(vt[b], jnp.exp2(scores[b] - top).astype(BF16))
+            ot = ot[:128] * (1.0 / ot[128:129])
             for h in range(4):
                 part = ot[32 * h : 32 * h + 32]
                 for j in range(4):
@@ -300,6 +311,7 @@
                     here = (lane128 >= to) & (lane128 < to + 16)
                     rows = slice(32 * h, 32 * h + 32)
                     tile[j // 2, rows] = jnp.where(here, moved, tile[j // 2, rows])
+            top = later_top
         for k in range(2):
             c = 2 * r + k
             go[c] = (tile[k] * gt[c]).astype(BF16)
@@ -311,8 +323,19 @@
                 push(go.at[c], gx.at[col], back_send, back_recv, row, c)
 
     loop(0, 8, block)
-    own = pltpu.make_async_copy(go.at[col], gx.at[col], keep.at[1])
-    own.start()
+    gx[col] = go[col]
+    take(gx.at[pl.ds(0, 15)], back_recv)
+
+    def store(g):
+        at = pl.ds(4 * g, 4)
+        return pltpu.make_async_copy(out.at[:, at], out_hbm.at[:, at], keep.at[g])
+
+    for g in range(4):
+        for s in range(4 * g, 4 * g + 4):
+            t = update[s] + dot(gx[s], att_out_ref[...], TN)
+            for b in range(4):
+                out[b, s] = t[32 * b : 32 * b + 32]
+        store(g).start()
     take(rx.at[0, pl.ds(0, 127)], right_send)
     take(rx.at[0, pl.ds(0, 127)], left_send)
     take(px.at[pl.ds(0, 127)], prod_send)
@@ -321,41 +344,15 @@
     take(bx.at[pl.ds(0, 12)], plane_send)
     take(bx.at[pl.ds(0, 48)], near_send)
     take(bx.at[pl.ds(0, 64)], far_send)
-    saved.wait()
-    own.wait()
     take(go.at[pl.ds(0, 15)], back_send)
-    take(go.at[pl.ds(0, 15)], back_recv)
-
-
-def final(gx_hbm, mid_hbm, att_out_ref, y_hbm, gx, mid, y, gx_sem, mid_sem, y_sem):
-    def fetch(g):
-        at = pl.ds(4 * g, 4)
-        return (
-            pltpu.make_async_copy(gx_hbm.at[at], gx.at[at], gx_sem.at[g]),
-            pltpu.make_async_copy(mid_hbm.at[at], mid.at[at], mid_sem.at[g]),
-        )
-
-    def store(g):
-        at = pl.ds(4 * g, 4)
-        return pltpu.make_async_copy(y.at[:, at], y_hbm.at[:, at], y_sem.at[g])
-
-    for g in range(4):
-        for copy in fetch(g):
-            copy.start()
-    for g in range(4):
-        for copy in fetch(g):
-            copy.wait()
-        for s in range(4 * g, 4 * g + 4):
-            out = mid[s] + dot(gx[s], att_out_ref[...], TN)
-            for b in range(4):
-                y[b, s] = out[32 * b : 32 * b + 32]
-        store(g).start()
     for g in range(4):
         store(g).wait()
 
 
 SCRATCH = [
     ((64, 32, 128), F32),
+    ((16, 128, 128), BF16),
+    ((4, 16, 32, 128), F32),
     ((16, 128, 128), F32),
     ((512, 128), BF16),
     ((128, 128), BF16),
@@ -380,44 +377,29 @@
     ((4, 144, 512), BF16),
     ((16, 128, 128), F32),
     ((8, 2, 32, 256), F32),
+    ((4, 512, 256), F32),
     ((2, 128, 128), F32),
     ((16, 128, 128), BF16),
 ]
-SEMAPHORES = [(), (), (), (), (8,), (), (), (), (), (), (), (), (), (), (8,), (), (8,), (), (), (2,)]
+SEMAPHORES = [(), (), (), (), (8,), (), (), (), (), (), (), (), (), (), (8,), (), (8,), (), (), (4,)]
 
 
 def per_device(pair, valid_length, tri_in, tri_gate, tri_out, att_in, att_bias, att_out):
     vmem = pl.BlockSpec(memory_space=pltpu.VMEM)
     smem = pl.BlockSpec(memory_space=pltpu.SMEM)
     anywhere = pl.BlockSpec(memory_space=pl.ANY)
-    middle, back = pl.pallas_call(
+    change = pl.pallas_call(
         kernel,
-        out_shape=[
-            jax.ShapeDtypeStruct((16, 128, 128), F32),
-            jax.ShapeDtypeStruct((16, 128, 128), BF16),
-        ],
-        in_specs=[anywhere, smem] + [vmem] * 5,
-        out_specs=[anywhere, anywhere],
+        out_shape=jax.ShapeDtypeStruct((4, 16, 32, 128), F32),
+        in_specs=[anywhere, smem] + [vmem] * 6,
+        out_specs=anywhere,
         scratch_shapes=[pltpu.VMEM(*s) for s in SCRATCH]
         + [pltpu.SemaphoreType.DMA(s) for s in SEMAPHORES],
         compiler_params=pltpu.CompilerParams(
             collective_id=0, has_side_effects=True, vmem_limit_bytes=60 * 1024 * 1024
         ),
-    )(pair, valid_length, tri_in, tri_gate, tri_out, att_bias.T, att_in)
-    out = pl.pallas_call(
-        final,
-        out_shape=jax.ShapeDtypeStruct((4, 16, 32, 128), F32),
-        in_specs=[anywhere, anywhere, vmem],
-        out_specs=anywhere,
-        scratch_shapes=[
-            pltpu.VMEM((16, 128, 128), BF16),
-            pltpu.VMEM((16, 128, 128), F32),
-            pltpu.VMEM((4, 16, 32, 128), F32),
-        ]
-        + [pltpu.SemaphoreType.DMA((4,))] * 3,
-        compiler_params=pltpu.CompilerParams(vmem_limit_bytes=60 * 1024 * 1024),
-    )(back, middle, att_out)
-    return out.reshape(64, 32, 128)
+    )(pair, valid_length, tri_in, tri_gate, tri_out, att_bias.T, att_in, att_out)
+    return pair + change.reshape(64, 32, 128)
 
 
 def solution(mesh):

time: 82.6 us -> 75.8 us (0.918); the launches traced: 81.3 us -> 75.4 us
  Pallas kernels: 80.6 us -> 72.3 us
  other arithmetic: 0 us -> 2.4 us
    pallas_call x2 -> x1, Pallas kernels: 80.6 us -> 72.3 us  [per_device(): pl.pallas_call(kernel, out_shape=jax.ShapeDtypeStruct((4, 16, 32, 128), F...]
    add x0 -> x1, other arithmetic: none -> 2.4 us  [per_device(): return pair + change.reshape(64, 32, 128)]
where the time goes in v5:
time: 75.8 us; the launch traced here: 75.4 us
  Pallas kernels  72.3 us (95%)
  other arithmetic  2.4 us (3%)
    pallas_call x1, Pallas kernels, per_device(): pl.pallas_call(kernel, out_shape=jax.ShapeDtypeStruct((4, 16, 32, 128), F...  72.3 us
    add x1, other arithmetic, per_device(): return pair + change.reshape(64, 32, 128)  2.4 us

profile of v5, /device:TPU:33, one launch (start us, length us, event | category | flops | bytes accessed | tf_op | source)
XLA Modules:
  0.0 75.4 jit_solution(17576976166827434415)
XLA Ops:
  0.7 0.0 copy-start
  0.7 72.3 %shard_map.82 = f32[4,16,32,128]{3,2,1,0:T(8,128)} custom-call(f32[64,32,128]{2,1,0:T(8,128)} %x_hbm.1, s32[1]{0:T(128)S(6)} %copy.9.len_ref, bf16[128,512]{1,0:T(8,128)(2,1)} %tri_in_ref.1, bf16[128,128]{1,0:T(8,128)(2,1)} %tri_gate_ref.1, bf16[128,128]{1,0:T(8,128)(2,1)} %tri_out_ref.1, bf16[4,128]{1,0:T(4,128)(2,1)} %bitcast.3, ...), custom_call_target="tpu_custom_call" | custom-call | tf_op jit(solution)/shard_map/pallas_call | solution.py:391
  73.0 0.0 copy-done
  73.0 2.4 %bitcast_add_fusion = f32[64,32,128]{2,1,0:T(8,128)} fusion(f32[64,32,128]{2,1,0:T(8,128)S(1)} %copy-done, f32[4,16,32,128]{3,2,1,0:T(8,128)} %shard_map.82), kind=kLoop, calls=%fused_computation | loop fusion | flops 262144 | bytes 3145728 | tf_op jit(solution)/shard_map/add | solution.py:402
Async XLA Ops:
  0.7 72.3 %copy-start = (f32[64,32,128]{2,1,0:T(8,128)S(1)}, f32[64,32,128]{2,1,0:T(8,128)}, u32[]{:S(2)}) copy-start(f32[64,32,128]{2,1,0:T(8,128)} %x_hbm.1) | copy-start | bytes 3145732

commit v6 on v5

--- a/solution.py
+++ b/solution.py
@@ -64,11 +64,11 @@
 
 
 def kernel(
-    x_hbm, len_ref, tri_in_ref, tri_gate_ref, tri_out_ref, bias_ref, att_in_ref, att_out_ref, out_hbm,
-    x_ref, gx, out, update, wt, wvt, wgt, y, e, rx, n, lm, rm, po, px, gate, np_, yb, nm, nx, bm, bx,
+    x_hbm, len_ref, tri_in_hbm, tri_gate_hbm, tri_out_hbm, bias_hbm, att_in_hbm, att_out_hbm, out,
+    x_ref, tri_in_ref, tri_gate_ref, tri_out_ref, bias_ref, att_in_ref, att_out_ref, gx, update, wt, wvt, wgt, y, e, rx, n, lm, rm, po, px, gate, np_, yb, nm, nx, bm, bx,
     qs, ks, vt, gt, bias, scores, tile, go,
     load, right_send, right_recv, left_send, left_recv, prod_send, prod_recv, norm_send, norm_recv,
-    line_send, line, plane_send, plane, near_send, near, far_send, far, back_send, back_recv, keep,
+    line_send, line, plane_send, plane, near_send, near, far_send, far, back_send, back_recv,
 ):
     row, col = lax.axis_index("row"), lax.axis_index("col")
     me = 16 * row + col
@@ -77,8 +77,13 @@
     y_at, z_at = row // 2, 2 * (row % 2) + z_lo
     mate = col + 1 - 2 * core
     bar = pltpu.get_barrier_semaphore()
-    fetch = pltpu.make_async_copy(x_hbm, x_ref, load)
-    fetch.start()
+    pairs = (
+        (tri_in_hbm, tri_in_ref), (x_hbm, x_ref), (tri_gate_hbm, tri_gate_ref), (att_in_hbm, att_in_ref),
+        (tri_out_hbm, tri_out_ref), (bias_hbm, bias_ref), (att_out_hbm, att_out_ref),
+    )
+    fetch = [pltpu.make_async_copy(a, b, load.at[n]) for n, (a, b) in enumerate(pairs)]
+    for copy in fetch:
+        copy.start()
 
     def greet(r, first=0):
         for k in range(first, 16):
@@ -87,12 +92,13 @@
 
     greet(row, 1)
     loop(1, 8, lambda a: greet(lax.rem(row + a, 8)))
+    fetch[0].wait()
     wt[...] = turned(tri_in_ref[...])
     perm = swap16()
     lane128 = lax.broadcasted_iota(jnp.int32, (1, 128), 1)
     length = len_ref[0]
     keep_k = (32 * col + lane128 % 32) < length
-    fetch.wait()
+    fetch[1].wait()
 
     def edge(side, s, nb):
         pt = dot(wt[256 * side : 256 * side + 256], nb, NT)
@@ -127,6 +133,8 @@
 
     loop(0, 16, first_edge, 4)
     order(1)
+    for copy in fetch[2:]:
+        copy.wait()
     pl.semaphore_wait(bar, 127)
     for q in range(4):
         send_right(2 * q)
@@ -326,16 +334,11 @@
     gx[col] = go[col]
     take(gx.at[pl.ds(0, 15)], back_recv)
 
-    def store(g):
-        at = pl.ds(4 * g, 4)
-        return pltpu.make_async_copy(out.at[:, at], out_hbm.at[:, at], keep.at[g])
-
     for g in range(4):
         for s in range(4 * g, 4 * g + 4):
             t = update[s] + dot(gx[s], att_out_ref[...], TN)
             for b in range(4):
                 out[b, s] = t[32 * b : 32 * b + 32]
-        store(g).start()
     take(rx.at[0, pl.ds(0, 127)], right_send)
     take(rx.at[0, pl.ds(0, 127)], left_send)
     take(px.at[pl.ds(0, 127)], prod_send)
@@ -345,14 +348,17 @@
     take(bx.at[pl.ds(0, 48)], near_send)
     take(bx.at[pl.ds(0, 64)], far_send)
     take(go.at[pl.ds(0, 15)], back_send)
-    for g in range(4):
-        store(g).wait()
 
 
 SCRATCH = [
     ((64, 32, 128), F32),
-    ((16, 128, 128), BF16),
-    ((4, 16, 32, 128), F32),
+    ((128, 512), BF16),
+    ((128, 128), BF16),
+    ((128, 128), BF16),
+    ((4, 128), BF16),
+    ((128, 512), BF16),
+    ((128, 128), BF16),
+    ((16, 128, 128), BF16),
     ((16, 128, 128), F32),
     ((512, 128), BF16),
     ((128, 128), BF16),
@@ -381,24 +387,24 @@
     ((2, 128, 128), F32),
     ((16, 128, 128), BF16),
 ]
-SEMAPHORES = [(), (), (), (), (8,), (), (), (), (), (), (), (), (), (), (8,), (), (8,), (), (), (4,)]
+SEMAPHORES = [(7,), (), (), (), (8,), (), (), (), (), (), (), (), (), (), (8,), (), (8,), (), ()]
 
 
 def per_device(pair, valid_length, tri_in, tri_gate, tri_out, att_in, att_bias, att_out):
     vmem = pl.BlockSpec(memory_space=pltpu.VMEM)
     smem = pl.BlockSpec(memory_space=pltpu.SMEM)
-    anywhere = pl.BlockSpec(memory_space=pl.ANY)
+    hbm = pl.BlockSpec(memory_space=pltpu.HBM)
     change = pl.pallas_call(
         kernel,
         out_shape=jax.ShapeDtypeStruct((4, 16, 32, 128), F32),
-        in_specs=[anywhere, smem] + [vmem] * 6,
-        out_specs=anywhere,
+        in_specs=[hbm, smem] + [hbm] * 6,
+        out_specs=vmem,
         scratch_shapes=[pltpu.VMEM(*s) for s in SCRATCH]
         + [pltpu.SemaphoreType.DMA(s) for s in SEMAPHORES],
         compiler_params=pltpu.CompilerParams(
-            collective_id=0, has_side_effects=True, vmem_limit_bytes=60 * 1024 * 1024
+            collective_id=0, has_side_effects=True, vmem_limit_bytes=40 * 1024 * 1024
         ),
-    )(pair, valid_length, tri_in, tri_gate, tri_out, att_bias.T, att_in, att_out)
+    )(*[a if n == 1 else pltpu.with_memory_space_constraint(a, pltpu.HBM) for n, a in enumerate((pair, valid_length, tri_in, tri_gate, tri_out, att_bias.T, att_in, att_out))])
     return pair + change.reshape(64, 32, 128)
 
 

time: 75.8 us -> 72.7 us (0.959)
  Pallas kernels: 72.3 us -> 70.6 us
  other arithmetic: 2.4 us -> 1.19 us
    pallas_call x1, Pallas kernels: 72.3 us -> 70.6 us  [per_device(): pl.pallas_call(kernel, out_shape=jax.ShapeDtypeStruct((4, 16, 32, 128), F...]
    add x1, other arithmetic: 2.4 us -> 1.19 us  [per_device(): return pair + change.reshape(64, 32, 128)]
where the time goes in v6:
time: 72.7 us; the launch traced here: 72.5 us
  Pallas kernels  70.6 us (97%)
  other arithmetic  1.19 us (2%)
    pallas_call x1, Pallas kernels, per_device(): pl.pallas_call(kernel, out_shape=jax.ShapeDtypeStruct((4, 16, 32, 128), F...  70.6 us

profile of v6, /device:TPU:33, one launch (start us, length us, event | category | flops | bytes accessed | tf_op | source)
XLA Modules:
  0.0 72.5 jit_solution(11740245831324422503)
XLA Ops:
  0.7 0.0 copy-start
  0.7 70.6 %shard_map.82 = f32[4,16,32,128]{3,2,1,0:T(8,128)S(1)} custom-call(f32[64,32,128]{2,1,0:T(8,128)} %x_hbm.1, s32[1]{0:T(128)S(6)} %copy.9.len_ref, bf16[128,512]{1,0:T(8,128)(2,1)} %tri_in_hbm.1, bf16[128,128]{1,0:T(8,128)(2,1)} %tri_gate_hbm.1, bf16[128,128]{1,0:T(8,128)(2,1)} %tri_out_hbm.1, bf16[4,128]{1,0:T(4,128)(2,1)} %bitcast.3, ...), custom_call_target="tpu_custom_call" | custom-call | tf_op jit(solution)/shard_map/pallas_call | solution.py:397
  71.3 0.0 copy-done
  71.3 1.2 %bitcast_add_fusion = f32[64,32,128]{2,1,0:T(8,128)} fusion(f32[64,32,128]{2,1,0:T(8,128)S(1)} %copy-done, f32[4,16,32,128]{3,2,1,0:T(8,128)S(1)} %shard_map.82), kind=kLoop, calls=%fused_computation | loop fusion | flops 262144 | bytes 3145728 | tf_op jit(solution)/shard_map/add | solution.py:408
Async XLA Ops:
  0.7 70.6 %copy-start = (f32[64,32,128]{2,1,0:T(8,128)S(1)}, f32[64,32,128]{2,1,0:T(8,128)}, u32[]{:S(2)}) copy-start(f32[64,32,128]{2,1,0:T(8,128)} %x_hbm.1) | copy-start | bytes 3145732

commit v7 on v6

--- a/solution.py
+++ b/solution.py
@@ -68,7 +68,7 @@
     x_ref, tri_in_ref, tri_gate_ref, tri_out_ref, bias_ref, att_in_ref, att_out_ref, gx, update, wt, wvt, wgt, y, e, rx, n, lm, rm, po, px, gate, np_, yb, nm, nx, bm, bx,
     qs, ks, vt, gt, bias, scores, tile, go,
     load, right_send, right_recv, left_send, left_recv, prod_send, prod_recv, norm_send, norm_recv,
-    line_send, line, plane_send, plane, near_send, near, far_send, far, back_send, back_recv,
+    line_send, line, plane_send, plane, early_send, early, near_send, near, far_send, far, back_send, back_recv,
 ):
     row, col = lax.axis_index("row"), lax.axis_index("col")
     me = 16 * row + col
@@ -115,9 +115,7 @@
             e[side, 32 * g + 16 : 32 * g + 32] = z[:, 128:].reshape(16, 16, 128)
 
     def first_edge(s):
-        nb = norm_last(tile_of(x_ref, s)).astype(BF16)
-        n[s] = nb
-        edge(1, s, nb)
+        edge(1, s, n[s])
 
     def send_right(a):
         r = lax.rem(row + a, 8)
@@ -131,6 +129,11 @@
             c = lax.rem(col + k, 16)
             push(e.at[0, 16 * r + c], rx.at[0, me], left_send, left_recv.at[a], r, c)
 
+    def first_norm(q):
+        rows = jnp.concatenate([tile_of(x_ref, 4 * q + k) for k in range(4)], axis=0)
+        n[pl.ds(pl.multiple_of(4 * q, 4), 4)] = norm_last(rows).astype(BF16).reshape(4, 128, 128)
+
+    loop(0, 4, first_norm, 4)
     loop(0, 16, first_edge, 4)
     order(1)
     for copy in fetch[2:]:
@@ -202,22 +205,22 @@
         def _():
             push(nm.at[s], nx.at[col], norm_send, norm_recv, row, s)
 
-    def middle(q):
-        first = 4 * lax.rem(q + 2 - 2 * z_lo, 4)
-        for s in [first + k for k in range(4)]:
+    for half in range(2):
+        first = 8 * (lax.rem(z_lo + 1, 2) if half == 0 else z_lo)
+        for s in [first + k for k in range(8)]:
             u = gate[s] * dot(np_[s], tri_out_ref[...], TN)
             update[s] = u
-            nb = norm_last(tile_of(x_ref, s) + u).astype(BF16)
-            nm[s] = nb
-            yb[pl.ds(s, 4, stride=16), :] = dot(wb, nb, NT)
-
-        @pl.when(q < 2)
-        def _():
+            gate[s] = tile_of(x_ref, s) + u
+        for q in range(2):
+            at = pl.ds(pl.multiple_of(first + 4 * q, 4), 4)
+            nb = norm_last(gate[at].reshape(512, 128)).astype(BF16)
+            nm[at] = nb.reshape(4, 128, 128)
+            z = dot(wb, nb, NT)
             for k in range(4):
-                s = first + k
-                push(nm.at[s], nx.at[col], norm_send, norm_recv, row, s)
-
-    loop(0, 4, middle)
+                yb[pl.ds(first + 4 * q + k, 4, stride=16), :] = z[:, 128 * k : 128 * k + 128]
+        for s in [first + k for k in range(8 if half == 0 else 0)]:
+            push(nm.at[s], nx.at[col], norm_send, norm_recv, row, s)
+
     yt = yb[...].T
     bm[...] = jnp.concatenate([yt[32 * b : 32 * b + 32] for b in range(4)], axis=1).astype(BF16)
     line_of = 64 * core + 8 * row + 4 * z_lo
@@ -229,16 +232,21 @@
     nx[col] = nm[col]
     bx[mine] = bm[...]
     take(bx.at[pl.ds(0, 3)], line)
+    z_hi = row % 2
     group = bx.at[pl.ds(line_of, 4)]
     for k in range(1, 4):
         z = lax.rem(z_at + k, 4)
         push(group, group, plane_send, plane, 2 * y_at + z // 2, 8 * (z % 2) + 2 * x_at + core)
+    for k in (1, 3, 2):
+        push(group, group, early_send, early.at[k], 2 * lax.rem(y_at + k, 4) + z_hi, col)
 
     def rows_of(o):
         turn = 2 * (x_at % 2)
-        back = jnp.where(o < 2, 0, jnp.where(o < 4, 1 + turn, jnp.where(o < 6, 3 - turn, 2)))
-        half = lax.rem(o + x_at, 2)
-        return 2 * lax.rem(y_at - back + 4, 4) + half, 2 * back + half
+        late = lax.rem(o + x_at // 2 + 2 * z_lo, 4)
+        last = jnp.where(late < 2, 3 - turn, 2)
+        back = jnp.where(o < 2, 0, jnp.where(o < 4, 1 + turn, last))
+        half = lax.rem(z_hi + jnp.where(o < 4, o, late), 2)
+        return 2 * lax.rem(y_at - back + 4, 4) + half, back, half == z_hi
 
     def bias_rows(r):
         return bx.at[pl.ds(64 * core + 8 * r, 8)]
@@ -247,11 +255,13 @@
     for o in range(2):
         mine_ = bias_rows(rows_of(o)[0])
         push(mine_, mine_, far_send, far.at[o], row, mate)
-    for half in range(2):
-        for k in (1, 3):
-            mine_ = bias_rows(2 * y_at + half)
-            r = 2 * lax.rem(y_at + k, 4) + row % 2
-            push(mine_, mine_, near_send, near.at[2 * k + half], r, col)
+    rest = bx.at[pl.ds(64 * core + 8 * row + 4 - 4 * z_lo, 4)]
+    whole = bias_rows(2 * y_at + 1 - z_hi)
+    for part in ((1, 3), (2,)):
+        for k in part:
+            push(rest, rest, near_send, near.at[k], 2 * lax.rem(y_at + k, 4) + z_hi, col)
+        for k in part:
+            push(whole, whole, near_send, near.at[4 + k], 2 * lax.rem(y_at + k, 4) + z_hi, col)
 
     kk = lax.broadcasted_iota(jnp.int32, (512, 256), 0)
     mask = jnp.where(kk < length, 0.0, -1e9).astype(F32).reshape(8, 2, 32, 256)
@@ -275,16 +285,19 @@
 
         @pl.when((o > 0) & (o < 7))
         def _():
-            later, slot = rows_of(o + 1)
+            later, back, own_half = rows_of(o + 1)
             rows = bias_rows(later)
-            take(bx.at[pl.ds(0, 8)], near.at[slot])
+
+            @pl.when(own_half)
+            def _():
+                take(bx.at[pl.ds(0, 4)], early.at[back])
+                take(bx.at[pl.ds(0, 4)], near.at[back])
+
+            @pl.when(jnp.logical_not(own_half))
+            def _():
+                take(bx.at[pl.ds(0, 8)], near.at[4 + back])
+
             push(rows, rows, far_send, far.at[o + 1], row, mate)
-            for k, half in ((1, 0), (3, 1)):
-
-                @pl.when(slot == 2 * k + half)
-                def _():
-                    to = 2 * lax.rem(y_at + k, 4) + row % 2
-                    push(rows, rows, near_send, near.at[4 + half], to, col)
 
         take(bx.at[pl.ds(0, 8)], far.at[o])
         for k in range(2):
@@ -345,7 +358,8 @@
     take(nx.at[pl.ds(0, 15)], norm_send)
     take(bx.at[pl.ds(0, 3)], line_send)
     take(bx.at[pl.ds(0, 12)], plane_send)
-    take(bx.at[pl.ds(0, 48)], near_send)
+    take(bx.at[pl.ds(0, 12)], early_send)
+    take(bx.at[pl.ds(0, 36)], near_send)
     take(bx.at[pl.ds(0, 64)], far_send)
     take(go.at[pl.ds(0, 15)], back_send)
 
@@ -387,7 +401,9 @@
     ((2, 128, 128), F32),
     ((16, 128, 128), BF16),
 ]
-SEMAPHORES = [(7,), (), (), (), (8,), (), (), (), (), (), (), (), (), (), (8,), (), (8,), (), ()]
+SEMAPHORES = [
+    (7,), (), (), (), (8,), (), (), (), (), (), (), (), (), (), (4,), (), (8,), (), (8,), (), (),
+]
 
 
 def per_device(pair, valid_length, tri_in, tri_gate, tri_out, att_in, att_bias, att_out):

time: 72.7 us -> 70.5 us (0.970)
  Pallas kernels: 70.6 us -> 68.5 us
    pallas_call x1, Pallas kernels: 70.6 us -> 68.5 us  [per_device(): pl.pallas_call(kernel, out_shape=jax.ShapeDtypeStruct((4, 16, 32, 128), F...]
where the time goes in v7:
time: 70.5 us; the launch traced here: 70.4 us
  Pallas kernels  68.5 us (97%)
  other arithmetic  1.19 us (2%)
    pallas_call x1, Pallas kernels, per_device(): pl.pallas_call(kernel, out_shape=jax.ShapeDtypeStruct((4, 16, 32, 128), F...  68.5 us

profile of v7, /device:TPU:33, one launch (start us, length us, event | category | flops | bytes accessed | tf_op | source)
XLA Modules:
  0.0 70.4 jit_solution(8678811171790938491)
XLA Ops:
  0.7 0.0 copy-start
  0.7 68.5 %shard_map.82 = f32[4,16,32,128]{3,2,1,0:T(8,128)S(1)} custom-call(f32[64,32,128]{2,1,0:T(8,128)} %x_hbm.1, s32[1]{0:T(128)S(6)} %copy.9.len_ref, bf16[128,512]{1,0:T(8,128)(2,1)} %tri_in_hbm.1, bf16[128,128]{1,0:T(8,128)(2,1)} %tri_gate_hbm.1, bf16[128,128]{1,0:T(8,128)(2,1)} %tri_out_hbm.1, bf16[4,128]{1,0:T(4,128)(2,1)} %bitcast.3, ...), custom_call_target="tpu_custom_call" | custom-call | tf_op jit(solution)/shard_map/pallas_call | solution.py:413
  69.2 0.0 copy-done
  69.2 1.2 %bitcast_add_fusion = f32[64,32,128]{2,1,0:T(8,128)} fusion(f32[64,32,128]{2,1,0:T(8,128)S(1)} %copy-done, f32[4,16,32,128]{3,2,1,0:T(8,128)S(1)} %shard_map.82), kind=kLoop, calls=%fused_computation | loop fusion | flops 262144 | bytes 3145728 | tf_op jit(solution)/shard_map/add | solution.py:424
Async XLA Ops:
  0.7 68.5 %copy-start = (f32[64,32,128]{2,1,0:T(8,128)S(1)}, f32[64,32,128]{2,1,0:T(8,128)}, u32[]{:S(2)}) copy-start(f32[64,32,128]{2,1,0:T(8,128)} %x_hbm.1) | copy-start | bytes 3145732

commit v8 on v7

--- a/solution.py
+++ b/solution.py
@@ -222,7 +222,9 @@
             push(nm.at[s], nx.at[col], norm_send, norm_recv, row, s)
 
     yt = yb[...].T
-    bm[...] = jnp.concatenate([yt[32 * b : 32 * b + 32] for b in range(4)], axis=1).astype(BF16)
+    own_keys = lax.broadcasted_iota(jnp.int32, (32, 256), 0) + 32 * col
+    yt = jnp.concatenate([yt[32 * b : 32 * b + 32] for b in range(4)], axis=1)
+    bm[...] = jnp.where(own_keys < length, yt, -1e9).astype(BF16)
     line_of = 64 * core + 8 * row + 4 * z_lo
     mine = line_of + x_at
     for k in range(1, 4):
@@ -236,35 +238,47 @@
     group = bx.at[pl.ds(line_of, 4)]
     for k in range(1, 4):
         z = lax.rem(z_at + k, 4)
-        push(group, group, plane_send, plane, 2 * y_at + z // 2, 8 * (z % 2) + 2 * x_at + core)
+        push(group, group, plane_send, plane.at[jnp.where(z // 2 == z_hi, 0, 1)], 2 * y_at + z // 2, 8 * (z % 2) + 2 * x_at + core)
     for k in (1, 3, 2):
         push(group, group, early_send, early.at[k], 2 * lax.rem(y_at + k, 4) + z_hi, col)
 
-    def rows_of(o):
-        turn = 2 * (x_at % 2)
-        late = lax.rem(o + x_at // 2 + 2 * z_lo, 4)
+    turn = 2 * (x_at % 2)
+    shift = x_at // 2 + 2 * z_lo
+
+    def listed(o):
+        late = lax.rem(o + shift, 4)
         last = jnp.where(late < 2, 3 - turn, 2)
         back = jnp.where(o < 2, 0, jnp.where(o < 4, 1 + turn, last))
         half = lax.rem(z_hi + jnp.where(o < 4, o, late), 2)
         return 2 * lax.rem(y_at - back + 4, 4) + half, back, half == z_hi
 
+    put_off = jnp.where(chip // 2 == y_at, lax.rem(chip + 4, 8), chip)
+    far_back = lax.rem(y_at - put_off // 2 + 4, 4)
+    other = jnp.where(put_off % 2 == z_hi, 0, 1)
+    place = jnp.where(
+        far_back == 1 + turn,
+        2 + other,
+        4 + lax.rem(other + jnp.where(far_back == 2, 2, 0) - shift + 4, 4),
+    )
+
+    def rows_of(o):
+        return listed(jnp.where(o == 7, place, o + jnp.where(o < place, 0, 1)))
+
     def bias_rows(r):
         return bx.at[pl.ds(64 * core + 8 * r, 8)]
 
-    take(bx.at[pl.ds(0, 12)], plane)
-    for o in range(2):
-        mine_ = bias_rows(rows_of(o)[0])
-        push(mine_, mine_, far_send, far.at[o], row, mate)
+    take(bx.at[pl.ds(0, 4)], plane.at[0])
     rest = bx.at[pl.ds(64 * core + 8 * row + 4 - 4 * z_lo, 4)]
-    whole = bias_rows(2 * y_at + 1 - z_hi)
-    for part in ((1, 3), (2,)):
-        for k in part:
-            push(rest, rest, near_send, near.at[k], 2 * lax.rem(y_at + k, 4) + z_hi, col)
-        for k in part:
-            push(whole, whole, near_send, near.at[4 + k], 2 * lax.rem(y_at + k, 4) + z_hi, col)
-
-    kk = lax.broadcasted_iota(jnp.int32, (512, 256), 0)
-    mask = jnp.where(kk < length, 0.0, -1e9).astype(F32).reshape(8, 2, 32, 256)
+    own_row, other_row = bias_rows(row), bias_rows(2 * y_at + 1 - z_hi)
+    push(own_row, own_row, far_send, far.at[0], row, mate)
+    for k in (1, 3, 2):
+        push(rest, rest, near_send, near.at[k], 2 * lax.rem(y_at + k, 4) + z_hi, col)
+
+    take(bx.at[pl.ds(0, 8)], plane.at[1])
+    push(other_row, other_row, far_send, far.at[1], row, mate)
+    for k in (1, 3, 2):
+        push(other_row, other_row, near_send, near.at[4 + k], 2 * lax.rem(y_at + k, 4) + z_hi, col)
+
     take(nx.at[pl.ds(0, 15)], norm_recv)
 
     def project(c):
@@ -278,6 +292,7 @@
     for b in range(4):
         vt[b, :128] = dot(wvt[...], nx[:, 32 * b : 32 * b + 32, :].reshape(512, 128), NT).astype(BF16)
         vt[b, 128:] = jnp.ones((16, 512), BF16)
+
     tile[...] = jnp.zeros((2, 128, 128), F32)
 
     def block(o):
@@ -302,7 +317,7 @@
         take(bx.at[pl.ds(0, 8)], far.at[o])
         for k in range(2):
             got = bx[pl.ds(pl.multiple_of(64 * k + 8 * r, 8), 8)].astype(F32)
-            bias[:, k] = (got + mask[:, k]) * LOG2E
+            bias[:, k] = got * LOG2E
 
         def score(b):
             q = qs[pl.ds(2 * r, 2), 32 * b : 32 * b + 32, :].reshape(4, 1, 16, 128)
@@ -402,7 +417,7 @@
     ((16, 128, 128), BF16),
 ]
 SEMAPHORES = [
-    (7,), (), (), (), (8,), (), (), (), (), (), (), (), (), (), (4,), (), (8,), (), (8,), (), (),
+    (7,), (), (), (), (8,), (), (), (), (), (), (), (), (2,), (), (4,), (), (8,), (), (8,), (), (),
 ]
 
 

time: 70.5 us -> 69.6 us (0.987)
  Pallas kernels: 68.5 us -> 67.3 us
    pallas_call x1, Pallas kernels: 68.5 us -> 67.3 us  [per_device(): pl.pallas_call(kernel, out_shape=jax.ShapeDtypeStruct((4, 16, 32, 128), F...]
where the time goes in v8:
time: 69.6 us; the launch traced here: 69.1 us
  Pallas kernels  67.3 us (97%)
  other arithmetic  1.19 us (2%)
    pallas_call x1, Pallas kernels, per_device(): pl.pallas_call(kernel, out_shape=jax.ShapeDtypeStruct((4, 16, 32, 128), F...  67.3 us

profile of v8, /device:TPU:33, one launch (start us, length us, event | category | flops | bytes accessed | tf_op | source)
XLA Modules:
  0.0 69.1 jit_solution(1154951557090111039)
XLA Ops:
  0.7 0.0 copy-start
  0.7 67.3 %shard_map.82 = f32[4,16,32,128]{3,2,1,0:T(8,128)S(1)} custom-call(f32[64,32,128]{2,1,0:T(8,128)} %x_hbm.1, s32[1]{0:T(128)S(6)} %copy.9.len_ref, bf16[128,512]{1,0:T(8,128)(2,1)} %tri_in_hbm.1, bf16[128,128]{1,0:T(8,128)(2,1)} %tri_gate_hbm.1, bf16[128,128]{1,0:T(8,128)(2,1)} %tri_out_hbm.1, bf16[4,128]{1,0:T(4,128)(2,1)} %bitcast.3, ...), custom_call_target="tpu_custom_call" | custom-call | tf_op jit(solution)/shard_map/pallas_call | solution.py:428
  67.9 0.0 copy-done
  67.9 1.2 %bitcast_add_fusion = f32[64,32,128]{2,1,0:T(8,128)} fusion(f32[64,32,128]{2,1,0:T(8,128)S(1)} %copy-done, f32[4,16,32,128]{3,2,1,0:T(8,128)S(1)} %shard_map.82), kind=kLoop, calls=%fused_computation | loop fusion | flops 262144 | bytes 3145728 | tf_op jit(solution)/shard_map/add | solution.py:439
Async XLA Ops:
  0.7 67.3 %copy-start = (f32[64,32,128]{2,1,0:T(8,128)S(1)}, f32[64,32,128]{2,1,0:T(8,128)}, u32[]{:S(2)}) copy-start(f32[64,32,128]{2,1,0:T(8,128)} %x_hbm.1) | copy-start | bytes 3145732

commit v9 on v8

--- a/solution.py
+++ b/solution.py
@@ -65,7 +65,7 @@
 
 def kernel(
     x_hbm, len_ref, tri_in_hbm, tri_gate_hbm, tri_out_hbm, bias_hbm, att_in_hbm, att_out_hbm, out,
-    x_ref, tri_in_ref, tri_gate_ref, tri_out_ref, bias_ref, att_in_ref, att_out_ref, gx, update, wt, wvt, wgt, y, e, rx, n, lm, rm, po, px, gate, np_, yb, nm, nx, bm, bx,
+    x_ref, tri_in_ref, tri_gate_ref, tri_out_ref, bias_ref, att_in_ref, att_out_ref, gx, update, wt, wvt, wgt, y, e, rx, n, lm, rm, po, px, gate, np_, stats, yb, nm, nx, bm, bx,
     qs, ks, vt, gt, bias, scores, tile, go,
     load, right_send, right_recv, left_send, left_recv, prod_send, prod_recv, norm_send, norm_recv,
     line_send, line, plane_send, plane, early_send, early, near_send, near, far_send, far, back_send, back_recv,
@@ -117,10 +117,10 @@
     def first_edge(s):
         edge(1, s, n[s])
 
-    def send_right(a):
-        r = lax.rem(row + a, 8)
-        for k in range(1 if a == 0 else 0, 16):
-            c = lax.rem(col + k, 16)
+    def send_right(k):
+        c = lax.rem(col + k, 16)
+        for a in range(1 if k == 0 else 0, 8):
+            r = lax.rem(row + a, 8)
             push(e.at[1, 16 * r + c], rx.at[1, me], right_send, right_recv, r, c)
 
     def send_left(a):
@@ -140,8 +140,8 @@
         copy.wait()
     pl.semaphore_wait(bar, 127)
     for q in range(4):
-        send_right(2 * q)
-        send_right(2 * q + 1)
+        for k in range(4):
+            send_right(4 * k + q)
         for s in range(4 * q, 4 * q + 4):
             edge(0, s, n[s])
     rx[1, me] = e[1, me]
@@ -175,29 +175,30 @@
                 po[16 * r + 4 * cg + c] = t
         for k in range(first, 16):
             c = lax.rem(col + k, 16)
-            push(po.at[16 * r + c], px.at[me], prod_send, prod_recv, r, c)
+            push(po.at[16 * r + c], px.at[me], prod_send, prod_recv.at[o], r, c)
 
     product(0, 1)
     loop(1, 8, product)
     px[me] = po[me]
-    take(px.at[pl.ds(0, 127)], prod_recv)
-
-    zero = jnp.zeros((16, 128), F32)
-    total = lax.fori_loop(0, 128, lambda c, a: a + px[c].astype(F32), zero, unroll=16)
-    mean = total * (1.0 / 128)
-
-    def square(c, a):
-        d = px[c].astype(F32) - mean
-        return a + d * d
-
-    scale = lax.rsqrt(lax.fori_loop(0, 128, square, zero, unroll=16) * (1.0 / 128) + 1e-5)
-
-    def normed(g):
-        z = ((px[rows16(g)].astype(F32) - mean[None]) * scale[None]).astype(BF16)
-        z = dot(perm, z.reshape(256, 128)).astype(BF16)
-        np_[:, rows16(g), :] = z.reshape(16, 16, 128)
-
-    loop(0, 8, normed, 4)
+
+    for o in range(8):
+        r = lax.rem(row - o + 8, 8)
+        take(px.at[pl.ds(0, 15 if o == 0 else 16)], prod_recv.at[o])
+        got = px[rows16(r)]
+        np_[:, rows16(r), :] = dot(perm, got.reshape(256, 128)).astype(BF16).reshape(16, 16, 128)
+        got = got.astype(F32)
+        group_mean = jnp.sum(got, axis=0) * (1.0 / 16)
+        got = got - group_mean[None]
+        squares = jnp.sum(got * got, axis=0)
+        if o == 0:
+            mean, spread = group_mean, squares
+        else:
+            step = group_mean - mean
+            mean = mean + step * (1.0 / (o + 1))
+            spread = spread + squares + step * step * (16.0 * o / (o + 1))
+    stats[0] = mean
+    stats[1] = lax.rsqrt(spread * (1.0 / 128) + 1e-5)
+
     wb = bias_ref[...]
 
     def send_norm(s):
@@ -208,7 +209,8 @@
     for half in range(2):
         first = 8 * (lax.rem(z_lo + 1, 2) if half == 0 else z_lo)
         for s in [first + k for k in range(8)]:
-            u = gate[s] * dot(np_[s], tri_out_ref[...], TN)
+            z = (np_[s].astype(F32) - stats[0, pl.ds(s, 1)]) * stats[1, pl.ds(s, 1)]
+            u = gate[s] * dot(z.astype(BF16), tri_out_ref[...], TN)
             update[s] = u
             gate[s] = tile_of(x_ref, s) + u
         for q in range(2):
@@ -281,14 +283,16 @@
 
     take(nx.at[pl.ds(0, 15)], norm_recv)
 
-    def project(c):
-        nb = nx[c]
+    for q in range(4):
+        at = slice(4 * q, 4 * q + 4)
+        nb = nx[at].reshape(512, 128)
         qk = dot(nb, att_in_ref[:, :256])
-        qs[c] = (qk[:, :128] * 32 ** (-0.5)).astype(BF16)
-        ks[c] = qk[:, 128:].astype(BF16)
-        gt[c] = jax.nn.sigmoid(dot(wgt[...], nb, NT))
-
-    loop(0, 16, project, 4)
+        qs[at] = (qk[:, :128] * 32 ** (-0.5)).astype(BF16).reshape(4, 128, 128)
+        ks[at] = qk[:, 128:].astype(BF16).reshape(4, 128, 128)
+    for q in range(4):
+        z = jax.nn.sigmoid(dot(wgt[...], nx[4 * q : 4 * q + 4].reshape(512, 128), NT))
+        for k in range(4):
+            gt[4 * q + k] = z[:, 128 * k : 128 * k + 128]
     for b in range(4):
         vt[b, :128] = dot(wvt[...], nx[:, 32 * b : 32 * b + 32, :].reshape(512, 128), NT).astype(BF16)
         vt[b, 128:] = jnp.ones((16, 512), BF16)
@@ -402,6 +406,7 @@
     ((128, 16, 128), BF16),
     ((16, 128, 128), F32),
     ((16, 128, 128), BF16),
+    ((2, 16, 128), F32),
     ((64, 128), F32),
     ((16, 128, 128), BF16),
     ((16, 128, 128), BF16),
@@ -417,7 +422,7 @@
     ((16, 128, 128), BF16),
 ]
 SEMAPHORES = [
-    (7,), (), (), (), (8,), (), (), (), (), (), (), (), (2,), (), (4,), (), (8,), (), (8,), (), (),
+    (7,), (), (), (), (8,), (), (8,), (), (), (), (), (), (2,), (), (4,), (), (8,), (), (8,), (), (),
 ]
 
 

time: 69.6 us -> 68.4 us (0.983)
  Pallas kernels: 67.3 us -> 65.8 us
    pallas_call x1, Pallas kernels: 67.3 us -> 65.8 us  [per_device(): pl.pallas_call(kernel, out_shape=jax.ShapeDtypeStruct((4, 16, 32, 128), F...]
where the time goes in v9:
time: 68.4 us; the launch traced here: 67.6 us
  Pallas kernels  65.8 us (96%)
  other arithmetic  1.19 us (2%)
    pallas_call x1, Pallas kernels, per_device(): pl.pallas_call(kernel, out_shape=jax.ShapeDtypeStruct((4, 16, 32, 128), F...  65.8 us

profile of v9, /device:TPU:33, one launch (start us, length us, event | category | flops | bytes accessed | tf_op | source)
XLA Modules:
  0.0 67.6 jit_solution(10576096373495780359)
XLA Ops:
  0.7 0.0 copy-start
  0.7 65.8 %shard_map.82 = f32[4,16,32,128]{3,2,1,0:T(8,128)S(1)} custom-call(f32[64,32,128]{2,1,0:T(8,128)} %x_hbm.1, s32[1]{0:T(128)S(6)} %copy.9.len_ref, bf16[128,512]{1,0:T(8,128)(2,1)} %tri_in_hbm.1, bf16[128,128]{1,0:T(8,128)(2,1)} %tri_gate_hbm.1, bf16[128,128]{1,0:T(8,128)(2,1)} %tri_out_hbm.1, bf16[4,128]{1,0:T(4,128)(2,1)} %bitcast.3, ...), custom_call_target="tpu_custom_call" | custom-call | tf_op jit(solution)/shard_map/pallas_call | solution.py:433
  66.4 0.0 copy-done
  66.4 1.2 %bitcast_add_fusion = f32[64,32,128]{2,1,0:T(8,128)} fusion(f32[64,32,128]{2,1,0:T(8,128)S(1)} %copy-done, f32[4,16,32,128]{3,2,1,0:T(8,128)S(1)} %shard_map.82), kind=kLoop, calls=%fused_computation | loop fusion | flops 262144 | bytes 3145728 | tf_op jit(solution)/shard_map/add | solution.py:444
Async XLA Ops:
  0.7 65.8 %copy-start = (f32[64,32,128]{2,1,0:T(8,128)S(1)}, f32[64,32,128]{2,1,0:T(8,128)}, u32[]{:S(2)}) copy-start(f32[64,32,128]{2,1,0:T(8,128)} %x_hbm.1) | copy-start | bytes 3145732

commit v10 on v9

--- a/solution.py
+++ b/solution.py
@@ -123,11 +123,13 @@
             r = lax.rem(row + a, 8)
             push(e.at[1, 16 * r + c], rx.at[1, me], right_send, right_recv, r, c)
 
-    def send_left(a):
-        r = lax.rem(row + 8 - a, 8)
-        for k in range(1 if a == 0 else 0, 16):
+    def send_left(q):
+        for k in [4 * (j % 4) + j // 4 for j in range(16)]:
             c = lax.rem(col + k, 16)
-            push(e.at[0, 16 * r + c], rx.at[0, me], left_send, left_recv.at[a], r, c)
+            for a in (2 * q, 2 * q + 1):
+                if a or k:
+                    r = lax.rem(row + 8 - a, 8)
+                    push(e.at[0, 16 * r + c], rx.at[0, me], left_send, left_recv.at[a], r, c)
 
     def first_norm(q):
         rows = jnp.concatenate([tile_of(x_ref, 4 * q + k) for k in range(4)], axis=0)
@@ -147,8 +149,7 @@
     rx[1, me] = e[1, me]
     order(0)
     for q in range(4):
-        send_left(2 * q)
-        send_left(2 * q + 1)
+        send_left(q)
         for s in range(4 * q, 4 * q + 4):
             gate[s] = jax.nn.sigmoid(dot(n[s], tri_gate_ref[...]))
     rx[0, me] = e[0, me]
@@ -173,7 +174,7 @@
             tiles = [p[16 * b : 16 * b + 16, 128 * cg : 128 * cg + 128] for b in range(4)]
             for c, t in enumerate(block_turn(tiles)):
                 po[16 * r + 4 * cg + c] = t
-        for k in range(first, 16):
+        for k in [4 * (j % 4) + j // 4 for j in range(first, 16)]:
             c = lax.rem(col + k, 16)
             push(po.at[16 * r + c], px.at[me], prod_send, prod_recv.at[o], r, c)
 

time: 68.4 us -> 68.4 us (level)
  no operation moved by 1% of the time
where the time goes in v10:
time: 68.4 us; the launch traced here: 67.6 us
  Pallas kernels  65.8 us (96%)
  other arithmetic  1.19 us (2%)
    pallas_call x1, Pallas kernels, per_device(): pl.pallas_call(kernel, out_shape=jax.ShapeDtypeStruct((4, 16, 32, 128), F...  65.8 us

profile of v10, /device:TPU:33, one launch (start us, length us, event | category | flops | bytes accessed | tf_op | source)
XLA Modules:
  0.0 67.6 jit_solution(12706134227088782224)
XLA Ops:
  0.7 0.0 copy-start
  0.7 65.8 %shard_map.82 = f32[4,16,32,128]{3,2,1,0:T(8,128)S(1)} custom-call(f32[64,32,128]{2,1,0:T(8,128)} %x_hbm.1, s32[1]{0:T(128)S(6)} %copy.9.len_ref, bf16[128,512]{1,0:T(8,128)(2,1)} %tri_in_hbm.1, bf16[128,128]{1,0:T(8,128)(2,1)} %tri_gate_hbm.1, bf16[128,128]{1,0:T(8,128)(2,1)} %tri_out_hbm.1, bf16[4,128]{1,0:T(4,128)(2,1)} %bitcast.3, ...), custom_call_target="tpu_custom_call" | custom-call | tf_op jit(solution)/shard_map/pallas_call | solution.py:434
  66.4 0.0 copy-done
  66.5 1.2 %bitcast_add_fusion = f32[64,32,128]{2,1,0:T(8,128)} fusion(f32[64,32,128]{2,1,0:T(8,128)S(1)} %copy-done, f32[4,16,32,128]{3,2,1,0:T(8,128)S(1)} %shard_map.82), kind=kLoop, calls=%fused_computation | loop fusion | flops 262144 | bytes 3145728 | tf_op jit(solution)/shard_map/add | solution.py:445
Async XLA Ops:
  0.7 65.8 %copy-start = (f32[64,32,128]{2,1,0:T(8,128)S(1)}, f32[64,32,128]{2,1,0:T(8,128)}, u32[]{:S(2)}) copy-start(f32[64,32,128]{2,1,0:T(8,128)} %x_hbm.1) | copy-start | bytes 3145732

commit v11 on v10

--- a/solution.py
+++ b/solution.py
@@ -90,8 +90,8 @@
             c = lax.rem(col + k, 16)
             pl.semaphore_signal(bar, inc=1, device_id=(r, c), device_id_type=MESH)
 
+    loop(2, 9, lambda a: greet(lax.rem(row + lax.rem(a + 2, 8) + jnp.where(a > 5, 1, 0), 8)))
     greet(row, 1)
-    loop(1, 8, lambda a: greet(lax.rem(row + a, 8)))
     fetch[0].wait()
     wt[...] = turned(tri_in_ref[...])
     perm = swap16()

time: 68.4 us -> 69 us (level)
  no operation moved by 1% of the time
where the time goes in v11:
time: 69 us; the launch traced here: 68.1 us
  Pallas kernels  66.3 us (96%)
  other arithmetic  1.19 us (2%)
    pallas_call x1, Pallas kernels, per_device(): pl.pallas_call(kernel, out_shape=jax.ShapeDtypeStruct((4, 16, 32, 128), F...  66.3 us

profile of v11, /device:TPU:33, one launch (start us, length us, event | category | flops | bytes accessed | tf_op | source)
XLA Modules:
  0.0 68.1 jit_solution(9073261811718360964)
XLA Ops:
  0.7 0.0 copy-start
  0.7 66.3 %shard_map.82 = f32[4,16,32,128]{3,2,1,0:T(8,128)S(1)} custom-call(f32[64,32,128]{2,1,0:T(8,128)} %x_hbm.1, s32[1]{0:T(128)S(6)} %copy.9.len_ref, bf16[128,512]{1,0:T(8,128)(2,1)} %tri_in_hbm.1, bf16[128,128]{1,0:T(8,128)(2,1)} %tri_gate_hbm.1, bf16[128,128]{1,0:T(8,128)(2,1)} %tri_out_hbm.1, bf16[4,128]{1,0:T(4,128)(2,1)} %bitcast.3, ...), custom_call_target="tpu_custom_call" | custom-call | tf_op jit(solution)/shard_map/pallas_call | solution.py:434
  66.9 0.0 copy-done
  66.9 1.2 %bitcast_add_fusion = f32[64,32,128]{2,1,0:T(8,128)} fusion(f32[64,32,128]{2,1,0:T(8,128)S(1)} %copy-done, f32[4,16,32,128]{3,2,1,0:T(8,128)S(1)} %shard_map.82), kind=kLoop, calls=%fused_computation | loop fusion | flops 262144 | bytes 3145728 | tf_op jit(solution)/shard_map/add | solution.py:445
Async XLA Ops:
  0.7 66.3 %copy-start = (f32[64,32,128]{2,1,0:T(8,128)S(1)}, f32[64,32,128]{2,1,0:T(8,128)}, u32[]{:S(2)}) copy-start(f32[64,32,128]{2,1,0:T(8,128)} %x_hbm.1) | copy-start | bytes 3145732
